TPU v7x, 1024 devices: a whole 4x4x32 slice. The times are simulated.
1024 devices in a mesh: dp: 32 (over y, x, core), expert: 32 (over z).
Axes of the slice: x: 4, y: 4, z: 32, core: 2. Of those that a mesh axis runs over, the one named last changes fastest.
Arguments:
- tokens_in: bfloat16 [131072, 2048], P(('dp', 'expert')), may hold values from -6 to 6
- out_grad: bfloat16 [131072, 2048], P(('dp', 'expert')), may hold values from -3 to 3
- expert_ids: int32 [131072, 8], P(('dp', 'expert')), may hold values from 0 to 127, all different within a row; in each aligned block of 128 rows (0 to 127, 128 to 255, ...) at most 16 rows name the same one
- rest_scores: float32 [131072, 8], P(('dp', 'expert')), may hold values from -60 to 60
- router_weight: bfloat16 [2048, 128], replicated, may hold values from -0.125 to 0.125
- down_weight: bfloat16 [32, 768, 2048], P('expert'), may hold values from -0.125 to 0.125
- saved_hidden: bfloat16 [32, 32, 32, 16, 768], P('dp', 'expert'), may hold values from -6 to 6
Outputs:
- token_grad: bfloat16 [131072, 2048], P(('dp', 'expert'))
- router_grad: float32 [2048, 128], P('dp', 'expert')
- down_grad: float32 [32, 768, 2048], P('expert', 'dp')
- hidden_grad: bfloat16 [32, 32, 32, 16, 768], P('dp', 'expert')
Inputs may be any that keep to these rules, and one draw needn't show every extreme that they name: `expert_ids`: each row names 8 different experts; among the 128 tokens of one device no expert is named more than 16 times, a bound that some block reaches.
All inputs are finite; a program needn't handle non-finite values.
Results may differ from a plain program's by a relative error of at most 0.024.
Values may be sent and summed in bfloat16 or wider, within the bound.
No kernel may reach another device: no remote copies, remote signals or barrier semaphores. Data moves between devices by JAX's collectives and lax.ppermute only.
A program may use at most 64 MiB of HBM per device.

v0:
```python
import math

import jax
import jax.numpy as jnp
from jax import lax
from jax.sharding import PartitionSpec as P


def in_one_piece(arrays, axis, split_dim, concat_dim, along):
    widths = [math.prod(a.shape[along:]) for a in arrays]
    both = jnp.concatenate(
        [a.reshape(*a.shape[:along], w) for a, w in zip(arrays, widths)], axis=along
    )
    out = lax.all_to_all(both, axis, split_axis=split_dim, concat_axis=concat_dim, tiled=True)
    parts = jnp.split(out, [sum(widths[:k]) for k in range(1, len(widths))], axis=along)
    return tuple((b.reshape(*out.shape[:along], *a.shape[along:]) for a, b in zip(arrays, parts)))


def in_blocks(value, dim, peers):
    before, after = (value.shape[:dim], value.shape[dim + 1 :])
    return jnp.moveaxis(value.reshape(*before, peers, -1, *after), dim, 0)


def sum_at_owner(value, axis, dim):
    parts = in_blocks(value, dim, lax.axis_size(axis))
    arrived = lax.all_to_all(parts, axis, split_axis=0, concat_axis=0, tiled=True)
    return arrived.astype(jnp.float32).sum(axis=0)


def slot_layout(ids_block, window, capacity):
    hit_mask = (ids_block[:, :, None] == jnp.arange(window, dtype=jnp.int32)[None, None, :]).astype(
        jnp.int32
    )
    chosen = jnp.sum(hit_mask, axis=1)
    before = jnp.cumsum(chosen, axis=0) - chosen
    placed = (chosen[None, :, :] == 1) & (
        before[None, :, :] == jnp.arange(capacity, dtype=jnp.int32)[:, None, None]
    )
    slot_table = jnp.transpose(placed, (2, 0, 1)).astype(jnp.float32)
    return (slot_table, hit_mask.astype(jnp.float32))


def shards(tokens_in, out_grad, expert_ids, rest_scores, router_weight, down_weight, saved_hidden):
    window = lax.axis_size("expert")
    capacity = saved_hidden.shape[3]
    sources = saved_hidden.shape[2]
    hidden_units = saved_hidden.shape[4]
    width = out_grad.shape[1]
    scored = router_weight.shape[1]
    logits = jnp.dot(tokens_in, router_weight, preferred_element_type=jnp.float32)
    all_mask = (
        expert_ids[:, :, None] == jnp.arange(scored, dtype=jnp.int32)[None, None, :]
    ).astype(jnp.float32)
    picked = jnp.sum(all_mask * logits[:, None, :], axis=2)
    gate_sel = jax.nn.softmax(picked, axis=1)
    slot_table, hit_mask = slot_layout(expert_ids, window, capacity)
    gate_each = jnp.einsum("tkw,tk->tw", hit_mask, gate_sel)
    sent_grad = jnp.einsum(
        "wct,td->wcd", slot_table.astype(jnp.bfloat16), out_grad, preferred_element_type=jnp.float32
    ).astype(jnp.bfloat16)
    sent_gate = jnp.einsum("wct,tw->wc", slot_table, gate_each).astype(jnp.bfloat16)
    got_grad, got_gate = in_one_piece((sent_grad, sent_gate), "expert", 0, 0, 2)
    slot_rows = got_grad.reshape(sources * capacity, width)
    gate_flat = got_gate.reshape(sources * capacity).astype(jnp.float32)
    weight_now = down_weight[0]
    raw_grad = lax.dot_general(
        slot_rows, weight_now, (((1,), (1,)), ((), ())), preferred_element_type=jnp.float32
    )
    hidden_flat = saved_hidden[0, 0].reshape(sources * capacity, hidden_units)
    hid_grad = (gate_flat[:, None] * raw_grad).astype(jnp.bfloat16)
    scores = jnp.sum(raw_grad * hidden_flat.astype(jnp.float32), axis=1).reshape(sources, capacity)
    scaled = (gate_flat[:, None] * slot_rows.astype(jnp.float32)).astype(jnp.bfloat16)
    down_grad = sum_at_owner(
        lax.dot_general(
            hidden_flat, scaled, (((0,), (0,)), ((), ())), preferred_element_type=jnp.float32
        ).astype(jnp.bfloat16),
        "dp",
        0,
    )
    returned = lax.all_to_all(scores, "expert", split_axis=0, concat_axis=0, tiled=True)
    per_token = jnp.einsum("wct,wc->tw", slot_table, returned)
    score_tok = jnp.einsum("tkw,tw->tk", hit_mask, per_token)
    score_all = jnp.where(expert_ids < window, score_tok, rest_scores)
    mean_part = jnp.sum(gate_sel * score_all, axis=1, keepdims=True)
    logit_sel = gate_sel * (score_all - mean_part)
    logit_bf = jnp.einsum("tke,tk->te", all_mask, logit_sel).astype(jnp.bfloat16)
    summed_rows = sum_at_owner(
        lax.dot_general(
            tokens_in, logit_bf, (((0,), (0,)), ((), ())), preferred_element_type=jnp.float32
        ).astype(jnp.bfloat16),
        "dp",
        0,
    )
    router_grad = sum_at_owner(summed_rows.astype(jnp.bfloat16), "expert", 1)
    token_grad = lax.dot_general(
        logit_bf, router_weight, (((1,), (1,)), ((), ())), preferred_element_type=jnp.float32
    ).astype(jnp.bfloat16)
    hidden_grad = hid_grad.reshape(1, 1, sources, capacity, hidden_units)
    return (token_grad, router_grad, down_grad[None], hidden_grad)


def solution(mesh):
    return jax.shard_map(
        shards,
        mesh=mesh,
        in_specs=(
            P(("dp", "expert"), None),
            P(("dp", "expert"), None),
            P(("dp", "expert"), None),
            P(("dp", "expert"), None),
            P(),
            P("expert", None, None),
            P("dp", "expert", None, None, None),
        ),
        out_specs=(
            P(("dp", "expert"), None),
            P("dp", "expert"),
            P("expert", "dp", None),
            P("dp", "expert", None, None, None),
        ),
        check_vma=False,
    )
```

profile of v0, /device:TPU:1, one launch (start us, length us, event | category | flops | bytes accessed | tf_op | source)
XLA Modules:
  0.0 381.8 jit_solution(3287037672318278038)
XLA Ops:
  0.6 0.0 copy-start
  0.6 0.9 convert_reduce_fusion.1
  1.5 0.1 copy.48
  1.6 0.8 copy.46
  2.4 0.2 reduce_window_sum.11
  2.6 0.1 copy.50
  2.6 1.5 fusion.25
  4.2 0.4 select_reduce_fusion
  4.6 0.1 reduce_max.9
  4.7 0.7 fusion.12
  5.5 0.2 select_reduce_fusion.1
  5.6 0.1 copy.67
  5.7 0.2 copy.51
  5.9 1.7 convolution_convert_fusion.1
  7.7 0.2 pad_maximum_fusion
  7.9 239.9 %all_to_all.32 = bf16[32,16,2049]{2,1,0:T(8,128)(2,1)S(1)} all-to-all(bf16[32,16,2049]{2,1,0:T(8,128)(2,1)S(1)} %pad_maximum_fusion), channel_id=1, replica_groups=mesh['dp'=32,'expert'=32] {'expert'}, dimensions={0} | all-to-all | bytes 4196352 | tf_op jit(solution)/shard_map/all_to_all | solution.py:14
  247.8 0.0 copy-start.1
  247.8 1.4 copy-done.1
  249.1 0.1 fusion.19
  249.3 0.1 reshape.71
  249.4 0.0 slice-start
  249.4 0.0 copy-start.4
  249.4 0.0 copy-done
  249.4 1.6 slice-done
  251.0 0.2 copy-done.4
  251.1 0.0 copy-start.2
  251.1 0.0 copy-start.3
  251.1 2.8 multiply_convert_fusion.1
  254.0 0.1 all_to_all.21
  254.1 0.6 convert.4
  254.7 3.8 %all-to-all-start.1 = ((bf16[32,1,16]{2,1,0:T(2,128)(2,1)}), bf16[32,1,16]{2,1,0:T(2,128)(2,1)S(1)}, u32[]{:S(2)}, u32[]{:S(2)}) async-start(bf16[32,1,16]{2,1,0:T(2,128)(2,1)} %convert.4), calls=%async_computation.1 | async-start | bytes 32768 | tf_op jit(solution)/shard_map/all_to_all | solution.py:80
  258.5 0.9 slice_convert_fusion
  259.5 0.2 copy.78
  259.7 20.0 %all-to-all-done.1 = bf16[32,1,16]{2,1,0:T(2,128)(2,1)S(1)} async-done(((bf16[32,1,16]{2,1,0:T(2,128)(2,1)}), bf16[32,1,16]{2,1,0:T(2,128)(2,1)S(1)}, u32[]{:S(2)}, u32[]{:S(2)}) %all-to-all-start.1) | async-done | bytes 1056 | tf_op jit(solution)/shard_map/all_to_all | solution.py:80
  279.7 0.2 fusion.7
  279.9 0.0 copy-done.2
  279.9 0.0 copy-done.3
  280.0 0.1 copy.75
  280.1 0.3 fusion.4
  280.5 2.2 fusion.2
  282.6 2.1 copy.53
  284.7 9.7 %all-to-all-start.2 = ((bf16[32,64,128]{2,1,0:T(8,128)(2,1)}), bf16[32,64,128]{2,1,0:T(8,128)(2,1)}, u32[]{:S(2)}, u32[]{:S(2)}) async-start(bf16[32,64,128]{2,1,0:T(8,128)(2,1)} %bitcast.73), calls=%async_computation.2 | async-start | bytes 1048576 | tf_op jit(solution)/shard_map/all_to_all | solution.py:26
  294.3 3.4 multiply_convert_fusion
  297.7 8.1 %all-to-all-done.2 = bf16[32,64,128]{2,1,0:T(8,128)(2,1)} async-done(((bf16[32,64,128]{2,1,0:T(8,128)(2,1)}), bf16[32,64,128]{2,1,0:T(8,128)(2,1)}, u32[]{:S(2)}, u32[]{:S(2)}) %all-to-all-start.2) | async-done | bytes 524320 | tf_op jit(solution)/shard_map/all_to_all | solution.py:26
  305.8 1.1 reduce_sum.80
  306.9 0.1 copy.54
  307.1 0.7 reshape.84
  307.8 3.8 %all-to-all-start.3 = ((bf16[32,2,128]{2,1,0:T(2,128)(2,1)}), bf16[32,2,128]{2,1,0:T(2,128)(2,1)S(1)}, u32[]{:S(2)}, u32[]{:S(2)}) async-start(bf16[32,2,128]{2,1,0:T(2,128)(2,1)} %reshape.84), calls=%async_computation.3 | async-start | bytes 32768 | tf_op jit(solution)/shard_map/all_to_all | solution.py:26
  311.6 5.3 %convolution_convert_fusion = bf16[2048,768]{0,1:T(8,128)(2,1)} fusion(bf16[512,2048]{1,0:T(8,128)(2,1)} %bitcast.72, bf16[512,768]{1,0:T(8,128)(2,1)} %bitcast.83), kind=kOutput, calls=%fused_computation.2 | convolution fusion | flops 1612185600 | bytes 6029312 | tf_op jit(solution)/shard_map/dot_general | solution.py:74
  316.9 15.9 %all-to-all-done.3 = bf16[32,2,128]{2,1,0:T(2,128)(2,1)S(1)} async-done(((bf16[32,2,128]{2,1,0:T(2,128)(2,1)}), bf16[32,2,128]{2,1,0:T(2,128)(2,1)S(1)}, u32[]{:S(2)}, u32[]{:S(2)}) %all-to-all-start.3) | async-done | bytes 16416 | tf_op jit(solution)/shard_map/all_to_all | solution.py:26
  332.8 6.0 %all-to-all-start.4 = ((bf16[32,24,2048]{2,1,0:T(8,128)(2,1)}), bf16[32,24,2048]{2,1,0:T(8,128)(2,1)}, u32[]{:S(2)}, u32[]{:S(2)}) async-start(bf16[32,24,2048]{2,1,0:T(8,128)(2,1)} %bitcast.71), calls=%async_computation.4 | async-start | bytes 6291456 | tf_op jit(solution)/shard_map/all_to_all | solution.py:26
  338.7 2.1 convolution_convert_fusion.3
  340.9 0.1 reshape.85
  341.0 0.6 convert_reduce_fusion.2
  341.6 37.1 %all-to-all-done.4 = bf16[32,24,2048]{2,1,0:T(8,128)(2,1)} async-done(((bf16[32,24,2048]{2,1,0:T(8,128)(2,1)}), bf16[32,24,2048]{2,1,0:T(8,128)(2,1)}, u32[]{:S(2)}, u32[]{:S(2)}) %all-to-all-start.4) | async-done | bytes 3145760 | tf_op jit(solution)/shard_map/all_to_all | solution.py:26
  378.7 3.2 convert_reduce_fusion
  (8 shorter events, 0.2 us)
Async XLA Ops:
  0.6 248.8 %copy-start = (bf16[1,768,2048]{2,1,0:T(8,128)(2,1)S(1)}, bf16[1,768,2048]{2,1,0:T(8,128)(2,1)}, u32[]{:S(2)}) copy-start(bf16[1,768,2048]{2,1,0:T(8,128)(2,1)} %param.12) | copy-start | bytes 9437188
  247.8 1.4 copy-start.1
  249.4 1.6 slice-start
  249.4 1.8 copy-start.4
  251.1 28.7 %copy-start.2 = (s32[128,8]{0,1:T(8,128)S(1)}, s32[128,8]{0,1:T(8,128)}, u32[]{:S(2)}) copy-start(s32[128,8]{0,1:T(8,128)} %param.9) | copy-start | bytes 12292
  251.1 28.8 %copy-start.3 = (f32[128,8]{0,1:T(8,128)S(1)}, f32[128,8]{0,1:T(8,128)}, u32[]{:S(2)}) copy-start(f32[128,8]{0,1:T(8,128)} %param.10) | copy-start | bytes 12292
  254.7 25.0 %all-to-all-start.1 = ((bf16[32,1,16]{2,1,0:T(2,128)(2,1)}), bf16[32,1,16]{2,1,0:T(2,128)(2,1)S(1)}, u32[]{:S(2)}, u32[]{:S(2)}) async-start(bf16[32,1,16]{2,1,0:T(2,128)(2,1)} %convert.4), calls=%async_computation.1 | async-start | bytes 32768 | tf_op jit(solution)/shard_map/all_to_all | solution.py:80
  284.7 21.1 %all-to-all-start.2 = ((bf16[32,64,128]{2,1,0:T(8,128)(2,1)}), bf16[32,64,128]{2,1,0:T(8,128)(2,1)}, u32[]{:S(2)}, u32[]{:S(2)}) async-start(bf16[32,64,128]{2,1,0:T(8,128)(2,1)} %bitcast.73), calls=%async_computation.2 | async-start | bytes 1048576 | tf_op jit(solution)/shard_map/all_to_all | solution.py:26
  307.8 25.0 %all-to-all-start.3 = ((bf16[32,2,128]{2,1,0:T(2,128)(2,1)}), bf16[32,2,128]{2,1,0:T(2,128)(2,1)S(1)}, u32[]{:S(2)}, u32[]{:S(2)}) async-start(bf16[32,2,128]{2,1,0:T(2,128)(2,1)} %reshape.84), calls=%async_computation.3 | async-start | bytes 32768 | tf_op jit(solution)/shard_map/all_to_all | solution.py:26
  332.8 45.9 %all-to-all-start.4 = ((bf16[32,24,2048]{2,1,0:T(8,128)(2,1)}), bf16[32,24,2048]{2,1,0:T(8,128)(2,1)}, u32[]{:S(2)}, u32[]{:S(2)}) async-start(bf16[32,24,2048]{2,1,0:T(8,128)(2,1)} %bitcast.71), calls=%async_computation.4 | async-start | bytes 6291456 | tf_op jit(solution)/shard_map/all_to_all | solution.py:26
where the time goes:
time: 383 us; the launch traced here: 382 us
  blocking collectives  240 us (63%)
  waiting for transfers between devices  81.1 us (21%)
  starting transfers between devices  23.3 us (6%)
  matrix products  16.2 us (4%)
  other arithmetic  12.7 us (3%)
  local copies, waits for them, and re-layouts  7.93 us (2%)
    all_to_all x1, blocking collectives, in_one_piece(): lax.all_to_all(both, axis, split_axis=split_dim, concat_axis=concat_dim,...  240 us
    all_to_all x3, waiting for transfers between devices, sum_at_owner(): lax.all_to_all(parts, axis, split_axis=0, concat_axis=0, tiled=True)  61.1 us
    all_to_all x1, waiting for transfers between devices, shards(): lax.all_to_all(scores, 'expert', split_axis=0, concat_axis=0, tiled=True)  20 us
    all_to_all x3, starting transfers between devices, sum_at_owner(): lax.all_to_all(parts, axis, split_axis=0, concat_axis=0, tiled=True)  19.4 us
  transfers between devices with their start and end apart: 4, of which 4 were waited for; matrix products, arithmetic and copies ran while one was open for 3% of the time, Pallas kernels for 0%

commit v1 on v0

v1 whole, which is shorter than its diff:
```python
import jax
import jax.numpy as jnp
from jax import lax
from jax.sharding import PartitionSpec as P


F32 = jnp.float32
BF16 = jnp.bfloat16
NEAR = 8


def in_blocks(value, dim, peers):
    before, after = (value.shape[:dim], value.shape[dim + 1 :])
    return jnp.moveaxis(value.reshape(*before, peers, -1, *after), dim, 0)


def sum_at_owner(value, axis, dim):
    parts = in_blocks(value, dim, lax.axis_size(axis))
    arrived = lax.all_to_all(parts, axis, split_axis=0, concat_axis=0, tiled=True)
    return arrived.astype(F32).sum(axis=0)


def turned(value, start):
    twice = jnp.concatenate([value, value], axis=0)
    return lax.dynamic_slice_in_dim(twice, start, value.shape[0], axis=0)


def shift(value, step):
    n = lax.axis_size("expert")
    return lax.ppermute(value, "expert", [(k, (k + step) % n) for k in range(n)])


def shift_by_core(value, step):
    rows, n = lax.axis_size("dp"), lax.axis_size("expert")
    pairs = []
    for i in range(rows):
        way = step if i % 2 == 0 else -step
        pairs += [(i * n + k, i * n + (k + way) % n) for k in range(n)]
    return lax.ppermute(value, ("dp", "expert"), pairs)


def picker(places, gates, tokens):
    at = lax.broadcasted_iota(jnp.int32, (*places.shape, tokens), places.ndim)
    hit = at == places.astype(jnp.int32)[..., None]
    return jnp.where(hit, gates[..., None], 0.0).astype(BF16)


def pick(table, rows):
    return lax.dot_general(
        table, rows, (((1,), (0,)), ((), ())), preferred_element_type=F32
    ).astype(BF16)


def through(rows, weight, hidden):
    raw = lax.dot_general(rows, weight, (((1,), (1,)), ((), ())), preferred_element_type=F32)
    return raw.astype(BF16), jnp.sum(raw * hidden.astype(F32), axis=1)


def across(hidden, rows):
    return lax.dot_general(hidden, rows, (((0,), (0,)), ((), ())), preferred_element_type=F32)


SIDE = 4


def from_peers(parts, mine, place, perm_of, count):
    total = lax.dynamic_index_in_dim(parts, mine, 0, keepdims=False).astype(F32)
    for step in range(1, count):
        out = lax.dynamic_index_in_dim(parts, (mine + step) % count, 0, keepdims=False)
        got = lax.ppermute(out, "dp", [(i, perm_of(i, step)) for i in range(place)])
        total = total + got.astype(F32)
    return total


def sum_over_cores(partial):
    size = lax.axis_size("dp")
    width = partial.shape[1]
    core = lax.axis_index("dp") % 2
    parts = jnp.moveaxis(partial.reshape(size // 2, 2, -1, width), 1, 0)
    return from_peers(parts, core, size, lambda i, step: i ^ 1, 2).astype(BF16)


def sum_over_chips(halves):
    size = lax.axis_size("dp")
    at = lax.axis_index("dp") // 2
    rows, width = halves.shape[1:]
    sides = size // 2 // SIDE

    def in_x(i, step):
        return (i // (2 * SIDE)) * 2 * SIDE + ((i // 2 % SIDE + step) % SIDE) * 2 + i % 2

    def in_y(i, step):
        return ((i // (2 * SIDE) + step) % sides) * 2 * SIDE + i % (2 * SIDE)

    by_x = jnp.moveaxis(halves.reshape(sides, SIDE, rows, width), 1, 0)
    row = from_peers(by_x, at % SIDE, size, in_x, SIDE).astype(BF16)
    return from_peers(row, at // SIDE, size, in_y, sides)


def shards(tokens_in, out_grad, expert_ids, rest_scores, router_weight, down_weight, saved_hidden):
    n = lax.axis_size("expert")
    me = lax.axis_index("expert")
    even = lax.axis_index("dp") % 2 == 0
    capacity = saved_hidden.shape[3]
    hidden_units = saved_hidden.shape[4]
    tokens, width = out_grad.shape
    scored = router_weight.shape[1]
    top = expert_ids.shape[1]

    up, down = [out_grad], [out_grad]
    for _ in range(1, NEAR + 1):
        up.append(shift(up[-1], 1))
        down.append(shift(down[-1], -1))

    ids_t = expert_ids.T
    rest_t = rest_scores.T
    expert_at = lax.broadcasted_iota(jnp.int32, (scored, tokens), 0)
    logits = lax.dot_general(
        router_weight, tokens_in, (((0,), (1,)), ((), ())), preferred_element_type=F32
    )
    chosen = jnp.zeros((scored, tokens), jnp.bool_)
    rest = jnp.zeros((scored, tokens), F32)
    for k in range(top):
        same = expert_at == ids_t[k][None, :]
        chosen = chosen | same
        rest = jnp.where(same, rest_t[k][None, :], rest)
    highest = jnp.max(jnp.where(chosen, logits, -jnp.inf), axis=0, keepdims=True)
    power = jnp.where(chosen, jnp.exp(logits - highest), 0.0)
    gate = power / jnp.sum(power, axis=0, keepdims=True)
    hit = chosen[:n]
    earlier = lax.broadcasted_iota(jnp.int32, (tokens, tokens), 0) < lax.broadcasted_iota(
        jnp.int32, (tokens, tokens), 1
    )
    before = lax.dot_general(
        hit.astype(BF16), earlier.astype(BF16), (((1,), (0,)), ((), ())), preferred_element_type=F32
    )
    slot = jnp.where(hit, before, -1.0)
    gate_sent = gate[:n].astype(BF16).astype(F32)
    token_at = lax.broadcasted_iota(jnp.int32, (n, tokens), 1).astype(F32)
    placed = slot[:, None, :] == jnp.arange(capacity, dtype=F32)[None, :, None]
    place = jnp.sum(jnp.where(placed, token_at[:, None, :], 0.0), axis=2)
    slot_gate = jnp.sum(jnp.where(placed, gate_sent[:, None, :], 0.0), axis=2)
    meta = jnp.concatenate([place, slot_gate], axis=1)
    far_up = turned(meta, (me + NEAR + 1) % n)[:NEAR]
    far_down = turned(meta, (me + n - 2 * NEAR) % n)[:NEAR][::-1]
    last = lax.broadcasted_iota(jnp.int32, far_up.shape, 0) == NEAR - 1
    far_up = jnp.where(last & ~even, 0.0, far_up)
    far_down = jnp.where(last & even, 0.0, far_down)
    peer = jnp.arange(n)[:, None, None]
    far = jnp.where(peer == (me + NEAR) % n, far_up[None], 0.0) + jnp.where(
        peer == (me + n - NEAR) % n, far_down[None], 0.0
    )
    note = jnp.concatenate([meta[:, None], far], axis=1).reshape(n, 1, -1)
    note = lax.all_to_all(note, "expert", split_axis=0, concat_axis=0, tiled=True)
    note = turned(note, me)
    note = note.reshape(n, NEAR + 1, 2, capacity)

    back = [(n - h) % n for h in range(NEAR + 1)]
    far_up_rows = pick(
        picker(note[back[NEAR], 1:, 0], note[back[NEAR], 1:, 1], tokens).reshape(-1, tokens), up[NEAR]
    ).reshape(NEAR, capacity, width)
    far_down_rows = pick(
        picker(note[NEAR, 1:, 0], note[NEAR, 1:, 1], tokens).reshape(-1, tokens), down[NEAR]
    ).reshape(NEAR, capacity, width)
    opposite = shift_by_core(jnp.where(even, far_up_rows[-1], far_down_rows[-1]), NEAR)
    far_from_below, far_from_above = {}, {}
    for j in range(NEAR - 1, 0, -1):
        far_from_below[j] = shift(far_up_rows[j - 1], j)
        far_from_above[j] = shift(far_down_rows[j - 1], -j)

    near_table = picker(note[:, 0, 0], note[:, 0, 1], tokens)
    near_rows = [pick(near_table[n - h], up[h]) for h in range(NEAR, 0, -1)]
    near_rows += [pick(near_table[h], down[h]) for h in range(NEAR + 1)]
    far_rows = [far_from_above[j] for j in range(1, NEAR)] + [opposite]
    far_rows += [far_from_below[j] for j in range(NEAR - 1, 0, -1)]
    near = jnp.concatenate(near_rows, axis=0)
    far = jnp.concatenate(far_rows, axis=0)
    cut = near.shape[0]

    hidden = turned(saved_hidden[0, 0], (me + n - NEAR) % n).reshape(n * capacity, hidden_units)
    hid_near, score_near = through(near, down_weight[0], hidden[:cut])
    far, score_near = lax.optimization_barrier((far, score_near))
    hid_far, score_far = through(far, down_weight[0], hidden[cut:])
    home = (NEAR + n - me) % n
    scores = jnp.concatenate([score_near, score_far], axis=0).reshape(n, 1, capacity)
    scores, far = lax.optimization_barrier((turned(scores, home), far))
    returned = lax.all_to_all(scores, "expert", split_axis=0, concat_axis=0, tiled=True)[:, 0]
    partial = (across(hidden[:cut], near) + across(hidden[cut:], far)).astype(BF16)
    halves = sum_over_cores(partial)
    down_grad = sum_over_chips(halves)
    hid_grad = jnp.concatenate([hid_near, hid_far], axis=0)
    hidden_grad = turned(hid_grad.reshape(n, capacity, hidden_units), home)

    there = jnp.sum(jnp.where(placed, returned[:, :, None], 0.0), axis=1)
    safe = jnp.where(gate_sent > 0.0, gate_sent, 1.0)
    there = jnp.where(gate_sent > 0.0, there * (gate[:n] / safe), 0.0)
    weighed = jnp.concatenate([there, (gate * rest)[n:]], axis=0)
    logit_grad = (weighed - gate * jnp.sum(weighed, axis=0, keepdims=True)).astype(BF16)
    share = lax.dot_general(
        tokens_in, logit_grad, (((0,), (1,)), ((), ())), preferred_element_type=F32
    ).astype(BF16)
    summed_rows = sum_at_owner(share, "dp", 0)
    router_grad = sum_at_owner(summed_rows.astype(BF16), "expert", 1)
    token_grad = lax.dot_general(
        logit_grad, router_weight, (((0,), (1,)), ((), ())), preferred_element_type=F32
    ).astype(BF16)
    return (token_grad, router_grad, down_grad[None], hidden_grad[None, None])


def solution(mesh):
    return jax.shard_map(
        shards,
        mesh=mesh,
        in_specs=(
            P(("dp", "expert"), None),
            P(("dp", "expert"), None),
            P(("dp", "expert"), None),
            P(("dp", "expert"), None),
            P(),
            P("expert", None, None),
            P("dp", "expert", None, None, None),
        ),
        out_specs=(
            P(("dp", "expert"), None),
            P("dp", "expert"),
            P("expert", "dp", None),
            P("dp", "expert", None, None, None),
        ),
        check_vma=False,
    )
```

time: 383 us -> 389 us (1.016)
  blocking collectives: 240 us -> 0 us
  starting transfers between devices: 23.3 us -> 196 us
  waiting for transfers between devices: 81.1 us -> 112 us
  matrix products: 16.2 us -> 35.8 us
  local copies, waits for them, and re-layouts: 7.93 us -> 22.3 us
    all_to_all x1 -> x0, blocking collectives: 240 us -> none  [in_one_piece(): lax.all_to_all(both, axis, split_axis=split_dim, concat_axis=concat_dim,...]
    ppermute x0 -> x38, starting transfers between devices: none -> 159 us  [the longest x30 130 us: shift(): lax.ppermute(value, 'expert', [(k, (k + step) % n) for k in range(n)])]
    ppermute x0 -> x38, waiting for transfers between devices: none -> 58.3 us  [the longest x30 55.7 us: shift(): lax.ppermute(value, 'expert', [(k, (k + step) % n) for k in range(n)])]
    all_to_all x3 -> x2, waiting for transfers between devices: 61.1 us -> 19 us  [sum_at_owner(): lax.all_to_all(parts, axis, split_axis=0, concat_axis=0, tiled=True)]
    dot_general x8 -> x27, matrix products: 16.2 us -> 35.8 us  [the longest x19 17.6 us: pick(): lax.dot_general(table, rows, (((1,), (0,)), ((), ())), preferred_element_...]
    all_to_all x0 -> x1, waiting for transfers between devices: none -> 14 us  [shards(): lax.all_to_all(note, 'expert', split_axis=0, concat_axis=0, tiled=True)]
    all_to_all x0 -> x1, starting transfers between devices: none -> 13.6 us  [shards(): lax.all_to_all(note, 'expert', split_axis=0, concat_axis=0, tiled=True)]
    all_to_all x1, starting transfers between devices: 3.83 us -> 11.6 us  [shards(): lax.all_to_all(scores, 'expert', split_axis=0, concat_axis=0, tiled=True)]
  transfers between devices with their start and end apart: 4 -> 42, of which waited for: 4 -> 15; matrix products, arithmetic and copies ran while one was open for 3% -> 16% of each run, Pallas kernels for 0% -> 0%
where the time goes in v1:
time: 389 us; the launch traced here: 384 us
  starting transfers between devices  196 us (50%)
  waiting for transfers between devices  112 us (29%)
  matrix products  35.8 us (9%)
  local copies, waits for them, and re-layouts  22.3 us (6%)
  other arithmetic  15.7 us (4%)
    ppermute x30, starting transfers between devices, shift(): lax.ppermute(value, 'expert', [(k, (k + step) % n) for k in range(n)])  130 us
    ppermute x30, waiting for transfers between devices, shift(): lax.ppermute(value, 'expert', [(k, (k + step) % n) for k in range(n)])  55.7 us
    ppermute x7, starting transfers between devices, from_peers(): got = lax.ppermute(out, 'dp', [(i, perm_of(i, step)) for i in range(place)])  24.4 us
    all_to_all x1, waiting for transfers between devices, shards(): lax.all_to_all(scores, 'expert', split_axis=0, concat_axis=0, tiled=True)  20.8 us
    all_to_all x2, waiting for transfers between devices, sum_at_owner(): lax.all_to_all(parts, axis, split_axis=0, concat_axis=0, tiled=True)  19 us
    dot_general x19, matrix products, pick(): lax.dot_general(table, rows, (((1,), (0,)), ((), ())), preferred_element_...  17.6 us
    all_to_all x1, waiting for transfers between devices, shards(): lax.all_to_all(note, 'expert', split_axis=0, concat_axis=0, tiled=True)  14 us
    all_to_all x1, starting transfers between devices, shards(): lax.all_to_all(note, 'expert', split_axis=0, concat_axis=0, tiled=True)  13.6 us
  transfers between devices with their start and end apart: 42, of which 15 were waited for; matrix products, arithmetic and copies ran while one was open for 16% of the time, Pallas kernels for 0%

profile of v1, /device:TPU:1, one launch (start us, length us, event | category | flops | bytes accessed | tf_op | source)
XLA Modules:
  0.0 384.3 jit_solution(13956573876999787025)
XLA Ops:
  0.7 4.6 %collective-permute-start.15 = (bf16[128,2048]{1,0:T(8,128)(2,1)}, bf16[128,2048]{1,0:T(8,128)(2,1)}, u32[]{:S(2)}, u32[]{:S(2)}) collective-permute-start(bf16[128,2048]{1,0:T(8,128)(2,1)} %param.8), channel_id=1, source_target_pairs={{0,1},{1,2},{2,3},{3,4},{4,5},{5,6},{6,7},{7,8},{8,9},{9,10},{10,1... | collective-permute-start | bytes 1572872 | tf_op jit(solution)/shard_map/ppermute | solution.py:30
  5.3 16.8 %collective-permute-start = (bf16[128,2048]{1,0:T(8,128)(2,1)}, bf16[128,2048]{1,0:T(8,128)(2,1)}, u32[]{:S(2)}, u32[]{:S(2)}) collective-permute-start(bf16[128,2048]{1,0:T(8,128)(2,1)} %param.8), channel_id=1, source_target_pairs={{0,31},{1,0},{2,1},{3,2},{4,3},{5,4},{6,5},{7,6},{8,7},{9,8},{10,9... | collective-permute-start | bytes 1572872 | tf_op jit(solution)/shard_map/ppermute | solution.py:30
  24.7 7.4 %collective-permute-done.15 = bf16[128,2048]{1,0:T(8,128)(2,1)} collective-permute-done((bf16[128,2048]{1,0:T(8,128)(2,1)}, bf16[128,2048]{1,0:T(8,128)(2,1)}, u32[]{:S(2)}, u32[]{:S(2)}) %collective-permute-start.15) | collective-permute-done | bytes 524320 | tf_op jit(solution)/shard_map/ppermute | solution.py:30
  32.1 1.9 collective-permute-start.16
  35.4 4.6 %collective-permute-start.1 = (bf16[128,2048]{1,0:T(8,128)(2,1)}, bf16[128,2048]{1,0:T(8,128)(2,1)S(1)}, u32[]{:S(2)}, u32[]{:S(2)}) collective-permute-start(bf16[128,2048]{1,0:T(8,128)(2,1)} %collective-permute-done), channel_id=1, source_target_pairs={{0,31},{1,0},{2,1},{3,2},{4,3},{5,4},{6,5},{7,6},{8,7},{9,8},{10,9... | collective-permute-start | bytes 1572872 | tf_op jit(solution)/shard_map/ppermute | solution.py:30
  39.9 7.7 %collective-permute-done.16 = bf16[128,2048]{1,0:T(8,128)(2,1)S(1)} collective-permute-done((bf16[128,2048]{1,0:T(8,128)(2,1)}, bf16[128,2048]{1,0:T(8,128)(2,1)S(1)}, u32[]{:S(2)}, u32[]{:S(2)}) %collective-permute-start.16) | collective-permute-done | bytes 524320 | tf_op jit(solution)/shard_map/ppermute | solution.py:30
  47.6 1.9 collective-permute-start.17
  50.3 4.8 %collective-permute-start.2 = (bf16[128,2048]{1,0:T(8,128)(2,1)S(1)}, bf16[128,2048]{1,0:T(8,128)(2,1)}, u32[]{:S(2)}, u32[]{:S(2)}) collective-permute-start(bf16[128,2048]{1,0:T(8,128)(2,1)S(1)} %collective-permute-done.1), channel_id=1, source_target_pairs={{0,31},{1,0},{2,1},{3,2},{4,3},{5,4},{6,5},{7,6},{8,7},{9,8},{10,9... | collective-permute-start | bytes 1572872 | tf_op jit(solution)/shard_map/ppermute | solution.py:30
  55.2 6.9 %collective-permute-done.17 = bf16[128,2048]{1,0:T(8,128)(2,1)S(1)} collective-permute-done((bf16[128,2048]{1,0:T(8,128)(2,1)S(1)}, bf16[128,2048]{1,0:T(8,128)(2,1)S(1)}, u32[]{:S(2)}, u32[]{:S(2)}) %collective-permute-start.17) | collective-permute-done | bytes 524320 | tf_op jit(solution)/shard_map/ppermute | solution.py:30
  62.1 1.9 collective-permute-start.18
  64.4 5.1 %collective-permute-start.3 = (bf16[128,2048]{1,0:T(8,128)(2,1)}, bf16[128,2048]{1,0:T(8,128)(2,1)}, u32[]{:S(2)}, u32[]{:S(2)}) collective-permute-start(bf16[128,2048]{1,0:T(8,128)(2,1)} %collective-permute-done.2), channel_id=1, source_target_pairs={{0,31},{1,0},{2,1},{3,2},{4,3},{5,4},{6,5},{7,6},{8,7},{9,8},{10,9... | collective-permute-start | bytes 1572872 | tf_op jit(solution)/shard_map/ppermute | solution.py:30
  69.5 6.3 %collective-permute-done.18 = bf16[128,2048]{1,0:T(8,128)(2,1)} collective-permute-done((bf16[128,2048]{1,0:T(8,128)(2,1)S(1)}, bf16[128,2048]{1,0:T(8,128)(2,1)}, u32[]{:S(2)}, u32[]{:S(2)}) %collective-permute-start.18) | collective-permute-done | bytes 524320 | tf_op jit(solution)/shard_map/ppermute | solution.py:30
  75.8 1.9 collective-permute-start.19
  78.0 5.1 %collective-permute-start.4 = (bf16[128,2048]{1,0:T(8,128)(2,1)}, bf16[128,2048]{1,0:T(8,128)(2,1)}, u32[]{:S(2)}, u32[]{:S(2)}) collective-permute-start(bf16[128,2048]{1,0:T(8,128)(2,1)} %collective-permute-done.3), channel_id=1, source_target_pairs={{0,31},{1,0},{2,1},{3,2},{4,3},{5,4},{6,5},{7,6},{8,7},{9,8},{10,9... | collective-permute-start | bytes 1572872 | tf_op jit(solution)/shard_map/ppermute | solution.py:30
  83.1 5.7 %collective-permute-done.19 = bf16[128,2048]{1,0:T(8,128)(2,1)} collective-permute-done((bf16[128,2048]{1,0:T(8,128)(2,1)}, bf16[128,2048]{1,0:T(8,128)(2,1)}, u32[]{:S(2)}, u32[]{:S(2)}) %collective-permute-start.19) | collective-permute-done | bytes 524320 | tf_op jit(solution)/shard_map/ppermute | solution.py:30
  88.9 1.9 collective-permute-start.20
  91.7 13.6 %all-to-all-start = ((f32[32,1,288]{2,1,0:T(1,128)}), f32[32,1,288]{2,1,0:T(1,128)}, u32[]{:S(2)}, u32[]{:S(2)}) async-start(f32[32,1,288]{2,1,0:T(1,128)} %copy.38), calls=%async_computation | async-start | bytes 98304 | tf_op jit(solution)/shard_map/all_to_all | solution.py:154
  105.3 4.4 %collective-permute-start.5 = (bf16[128,2048]{1,0:T(8,128)(2,1)}, bf16[128,2048]{1,0:T(8,128)(2,1)}, u32[]{:S(2)}, u32[]{:S(2)}) collective-permute-start(bf16[128,2048]{1,0:T(8,128)(2,1)} %collective-permute-done.4), channel_id=1, source_target_pairs={{0,31},{1,0},{2,1},{3,2},{4,3},{5,4},{6,5},{7,6},{8,7},{9,8},{10,9... | collective-permute-start | bytes 1572872 | tf_op jit(solution)/shard_map/ppermute | solution.py:30
  109.7 1.9 collective-permute-start.21
  114.0 14.0 %all-to-all-done = f32[32,1,288]{2,1,0:T(1,128)} async-done(((f32[32,1,288]{2,1,0:T(1,128)}), f32[32,1,288]{2,1,0:T(1,128)}, u32[]{:S(2)}, u32[]{:S(2)}) %all-to-all-start) | async-done | bytes 36896 | tf_op jit(solution)/shard_map/all_to_all | solution.py:154
  130.7 1.9 collective-permute-start.6
  132.6 3.4 collective-permute-start.22
  137.4 2.0 fusion.32
  146.4 3.1 collective-permute-start.7
  159.5 2.1 collective-permute-start.8
  169.4 4.5 %fusion.66 = f32[768,2048]{1,0:T(8,128)} fusion(bf16[272,768]{1,0:T(8,128)(2,1)S(1)} %bitcast.184, bf16[272,2048]{1,0:T(8,128)(2,1)S(1)} %fusion.6), kind=kOutput, calls=%fused_computation.207 | convolution fusion | flops 855638016 | bytes 7823360 | tf_op jit(solution)/shard_map/dot_general | solution.py:60
  174.0 1.8 fusion.63
  175.8 1.9 collective-permute-start.9
  177.7 2.6 collective-permute-start.10
  180.3 4.5 %collective-permute-start.11 = (bf16[16,2048]{1,0:T(8,128)(2,1)S(1)}, bf16[16,2048]{1,0:T(8,128)(2,1)S(1)}, u32[]{:S(2)}, u32[]{:S(2)}) collective-permute-start(bf16[16,2048]{1,0:T(8,128)(2,1)S(1)} %get-tuple-element.40), channel_id=1, source_target_pairs={{0,28},{1,29},{2,30},{3,31},{4,0},{5,1},{6,2},{7,3},{8,4},{9,5},{1... | collective-permute-start | bytes 196616 | tf_op jit(solution)/shard_map/ppermute | solution.py:30
  184.8 7.1 %collective-permute-start.12 = (bf16[16,2048]{1,0:T(8,128)(2,1)S(1)}, bf16[16,2048]{1,0:T(8,128)(2,1)S(1)}, u32[]{:S(2)}, u32[]{:S(2)}) collective-permute-start(bf16[16,2048]{1,0:T(8,128)(2,1)S(1)} %get-tuple-element.39), channel_id=1, source_target_pairs={{0,27},{1,28},{2,29},{3,30},{4,31},{5,0},{6,1},{7,2},{8,3},{9,4},{... | collective-permute-start | bytes 196616 | tf_op jit(solution)/shard_map/ppermute | solution.py:30
  191.9 5.4 %collective-permute-start.13 = (bf16[16,2048]{1,0:T(8,128)(2,1)S(1)}, bf16[16,2048]{1,0:T(8,128)(2,1)S(1)}, u32[]{:S(2)}, u32[]{:S(2)}) collective-permute-start(bf16[16,2048]{1,0:T(8,128)(2,1)S(1)} %get-tuple-element.38), channel_id=1, source_target_pairs={{0,26},{1,27},{2,28},{3,29},{4,30},{5,31},{6,0},{7,1},{8,2},{9,3},... | collective-permute-start | bytes 196616 | tf_op jit(solution)/shard_map/ppermute | solution.py:30
  197.3 8.9 %collective-permute-start.14 = (bf16[16,2048]{1,0:T(8,128)(2,1)S(1)}, bf16[16,2048]{1,0:T(8,128)(2,1)S(1)}, u32[]{:S(2)}, u32[]{:S(2)}) collective-permute-start(bf16[16,2048]{1,0:T(8,128)(2,1)S(1)} %get-tuple-element.37), channel_id=1, source_target_pairs={{0,25},{1,26},{2,27},{3,28},{4,29},{5,30},{6,31},{7,0},{8,1},{9,2}... | collective-permute-start | bytes 196616 | tf_op jit(solution)/shard_map/ppermute | solution.py:30
  206.1 4.7 %collective-permute-start.23 = (bf16[16,2048]{1,0:T(8,128)(2,1)S(1)}, bf16[16,2048]{1,0:T(8,128)(2,1)S(1)}, u32[]{:S(2)}, u32[]{:S(2)}) collective-permute-start(bf16[16,2048]{1,0:T(8,128)(2,1)S(1)} %get-tuple-element.36), channel_id=1, source_target_pairs={{0,8},{1,9},{2,10},{3,11},{4,12},{5,13},{6,14},{7,15},{8,16},{9,17... | collective-permute-start | bytes 196616 | tf_op jit(solution)/shard_map/ppermute | solution.py:39
  210.9 6.9 %collective-permute-start.24 = (bf16[16,2048]{1,0:T(8,128)(2,1)S(1)}, bf16[16,2048]{1,0:T(8,128)(2,1)S(1)}, u32[]{:S(2)}, u32[]{:S(2)}) collective-permute-start(bf16[16,2048]{1,0:T(8,128)(2,1)S(1)} %get-tuple-element.35), channel_id=1, source_target_pairs={{0,7},{1,8},{2,9},{3,10},{4,11},{5,12},{6,13},{7,14},{8,15},{9,16}... | collective-permute-start | bytes 196616 | tf_op jit(solution)/shard_map/ppermute | solution.py:30
  217.8 3.6 collective-permute-start.25
  221.5 6.8 %collective-permute-start.26 = (bf16[16,2048]{1,0:T(8,128)(2,1)S(1)}, bf16[16,2048]{1,0:T(8,128)(2,1)S(1)}, u32[]{:S(2)}, u32[]{:S(2)}) collective-permute-start(bf16[16,2048]{1,0:T(8,128)(2,1)S(1)} %get-tuple-element.33), channel_id=1, source_target_pairs={{0,5},{1,6},{2,7},{3,8},{4,9},{5,10},{6,11},{7,12},{8,13},{9,14},{... | collective-permute-start | bytes 196616 | tf_op jit(solution)/shard_map/ppermute | solution.py:30
  228.3 4.3 %collective-permute-start.27 = (bf16[16,2048]{1,0:T(8,128)(2,1)S(1)}, bf16[16,2048]{1,0:T(8,128)(2,1)S(1)}, u32[]{:S(2)}, u32[]{:S(2)}) collective-permute-start(bf16[16,2048]{1,0:T(8,128)(2,1)S(1)} %get-tuple-element.32), channel_id=1, source_target_pairs={{0,4},{1,5},{2,6},{3,7},{4,8},{5,9},{6,10},{7,11},{8,12},{9,13},{1... | collective-permute-start | bytes 196616 | tf_op jit(solution)/shard_map/ppermute | solution.py:30
  232.9 3.7 collective-permute-start.28
  236.7 3.4 collective-permute-start.29
  240.1 3.2 collective-permute-start.30
  243.4 5.2 %collective-permute-done.26 = bf16[16,2048]{1,0:T(8,128)(2,1)S(1)} collective-permute-done((bf16[16,2048]{1,0:T(8,128)(2,1)S(1)}, bf16[16,2048]{1,0:T(8,128)(2,1)S(1)}, u32[]{:S(2)}, u32[]{:S(2)}) %collective-permute-start.26) | collective-permute-done | bytes 65568 | tf_op jit(solution)/shard_map/ppermute | solution.py:30
  248.5 4.9 %collective-permute-done.27 = bf16[16,2048]{1,0:T(8,128)(2,1)S(1)} collective-permute-done((bf16[16,2048]{1,0:T(8,128)(2,1)S(1)}, bf16[16,2048]{1,0:T(8,128)(2,1)S(1)}, u32[]{:S(2)}, u32[]{:S(2)}) %collective-permute-start.27) | collective-permute-done | bytes 65568 | tf_op jit(solution)/shard_map/ppermute | solution.py:30
  253.4 8.2 %collective-permute-done.28 = bf16[16,2048]{1,0:T(8,128)(2,1)S(1)} collective-permute-done((bf16[16,2048]{1,0:T(8,128)(2,1)S(1)}, bf16[16,2048]{1,0:T(8,128)(2,1)S(1)}, u32[]{:S(2)}, u32[]{:S(2)}) %collective-permute-start.28) | collective-permute-done | bytes 65568 | tf_op jit(solution)/shard_map/ppermute | solution.py:30
  261.7 3.4 collective-permute-done.30
  265.1 1.8 fusion.64
  267.7 4.1 %add_convert_fusion = bf16[768,2048]{1,0:T(8,128)(2,1)S(1)} fusion(f32[768,2048]{1,0:T(8,128)} %fusion.66, bf16[240,768]{1,0:T(8,128)(2,1)S(1)} %bitcast.188, bf16[240,2048]{1,0:T(8,128)(2,1)} %copy-done.5), kind=kOutput, calls=%fused_computation | convolution fusion | flops 758120448 | bytes 10788864 | tf_op jit(solution)/shard_map/dot_general | solution.py:60
  273.9 3.3 collective-permute-start.31
  277.2 11.6 %all-to-all-start.1 = ((f32[32,1,16]{2,1,0:T(1,128)}), f32[32,1,16]{2,1,0:T(1,128)S(1)}, u32[]{:S(2)}, u32[]{:S(2)}) async-start(f32[32,1,16]{2,1,0:T(1,128)} %bitcast.35), calls=%async_computation.1 | async-start | bytes 32768 | tf_op jit(solution)/shard_map/all_to_all | solution.py:187
  289.2 20.8 %all-to-all-done.1 = f32[32,1,16]{2,1,0:T(1,128)S(1)} async-done(((f32[32,1,16]{2,1,0:T(1,128)}), f32[32,1,16]{2,1,0:T(1,128)S(1)}, u32[]{:S(2)}, u32[]{:S(2)}) %all-to-all-start.1) | async-done | bytes 2080 | tf_op jit(solution)/shard_map/all_to_all | solution.py:187
  310.8 2.1 fusion.5
  312.9 2.1 copy.44
  315.0 8.6 %all-to-all-start.2 = ((bf16[32,64,128]{2,1,0:T(8,128)(2,1)}), bf16[32,64,128]{2,1,0:T(8,128)(2,1)}, u32[]{:S(2)}, u32[]{:S(2)}) async-start(bf16[32,64,128]{2,1,0:T(8,128)(2,1)} %bitcast.186), calls=%async_computation.2 | async-start | bytes 1048576 | tf_op jit(solution)/shard_map/all_to_all | solution.py:19
  323.6 2.5 fusion
  327.6 3.2 collective-permute-start.32
  330.8 4.3 %collective-permute-start.33 = (bf16[4,24,2048]{2,1,0:T(8,128)(2,1)}, bf16[4,24,2048]{2,1,0:T(8,128)(2,1)}, u32[]{:S(2)}, u32[]{:S(2)}) collective-permute-start(bf16[4,24,2048]{2,1,0:T(8,128)(2,1)} %get-tuple-element.24), channel_id=1, source_target_pairs={{0,128},{32,160},{64,192},{96,224},{128,0},{160,32},{192,64},{224,... | collective-permute-start | bytes 1179656 | tf_op jit(solution)/shard_map/ppermute | solution.py:70
  335.1 3.1 collective-permute-start.34
  342.8 3.8 all-to-all-start.3
  346.7 2.2 convolution_convert_fusion.1
  348.8 19.0 %all-to-all-done.3 = bf16[32,2,128]{2,1,0:T(2,128)(2,1)S(1)} async-done(((bf16[32,2,128]{2,1,0:T(2,128)(2,1)}), bf16[32,2,128]{2,1,0:T(2,128)(2,1)S(1)}, u32[]{:S(2)}, u32[]{:S(2)}) %all-to-all-start.3) | async-done | bytes 16416 | tf_op jit(solution)/shard_map/all_to_all | solution.py:19
  370.2 3.1 collective-permute-start.35
  373.3 4.4 %collective-permute-start.36 = (bf16[24,2048]{1,0:T(8,128)(2,1)S(1)}, bf16[24,2048]{1,0:T(8,128)(2,1)S(1)}, u32[]{:S(2)}, u32[]{:S(2)}) collective-permute-start(bf16[24,2048]{1,0:T(8,128)(2,1)S(1)} %get-tuple-element.46), channel_id=1, source_target_pairs={{0,512},{32,544},{64,576},{96,608},{128,640},{160,672},{192,704},{... | collective-permute-start | bytes 294920 | tf_op jit(solution)/shard_map/ppermute | solution.py:70
  377.7 3.0 collective-permute-start.37
  381.4 2.2 collective-permute-done.37
  (191 shorter events, 51.2 us)
Async XLA Ops:
  0.6 173.3 %copy-start = (bf16[1,768,2048]{2,1,0:T(8,128)(2,1)S(1)}, bf16[1,768,2048]{2,1,0:T(8,128)(2,1)}, u32[]{:S(2)}) copy-start(bf16[1,768,2048]{2,1,0:T(8,128)(2,1)} %param.12) | copy-start | bytes 9437188
  0.6 33.4 %copy-start.25 = (f32[128,8]{0,1:T(8,128)S(1)}, f32[128,8]{0,1:T(8,128)}, u32[]{:S(2)}) copy-start(f32[128,8]{0,1:T(8,128)} %param.10) | copy-start | bytes 12292
  0.7 31.4 %collective-permute-start.15 = (bf16[128,2048]{1,0:T(8,128)(2,1)}, bf16[128,2048]{1,0:T(8,128)(2,1)}, u32[]{:S(2)}, u32[]{:S(2)}) collective-permute-start(bf16[128,2048]{1,0:T(8,128)(2,1)} %param.8), channel_id=1, source_target_pairs={{0,1},{1,2},{2,3},{3,4},{4,5},{5,6},{6,7},{7,8},{8,9},{9,10},{10,1... | collective-permute-start | bytes 1572872 | tf_op jit(solution)/shard_map/ppermute | solution.py:30
  5.3 30.1 %collective-permute-start = (bf16[128,2048]{1,0:T(8,128)(2,1)}, bf16[128,2048]{1,0:T(8,128)(2,1)}, u32[]{:S(2)}, u32[]{:S(2)}) collective-permute-start(bf16[128,2048]{1,0:T(8,128)(2,1)} %param.8), channel_id=1, source_target_pairs={{0,31},{1,0},{2,1},{3,2},{4,3},{5,4},{6,5},{7,6},{8,7},{9,8},{10,9... | collective-permute-start | bytes 1572872 | tf_op jit(solution)/shard_map/ppermute | solution.py:30
  32.1 15.5 %collective-permute-start.16 = (bf16[128,2048]{1,0:T(8,128)(2,1)}, bf16[128,2048]{1,0:T(8,128)(2,1)S(1)}, u32[]{:S(2)}, u32[]{:S(2)}) collective-permute-start(bf16[128,2048]{1,0:T(8,128)(2,1)} %collective-permute-done.15), channel_id=1, source_target_pairs={{0,1},{1,2},{2,3},{3,4},{4,5},{5,6},{6,7},{7,8},{8,9},{9,10},{10,1... | collective-permute-start | bytes 1572872 | tf_op jit(solution)/shard_map/ppermute | solution.py:30
  35.4 15.0 %collective-permute-start.1 = (bf16[128,2048]{1,0:T(8,128)(2,1)}, bf16[128,2048]{1,0:T(8,128)(2,1)S(1)}, u32[]{:S(2)}, u32[]{:S(2)}) collective-permute-start(bf16[128,2048]{1,0:T(8,128)(2,1)} %collective-permute-done), channel_id=1, source_target_pairs={{0,31},{1,0},{2,1},{3,2},{4,3},{5,4},{6,5},{7,6},{8,7},{9,8},{10,9... | collective-permute-start | bytes 1572872 | tf_op jit(solution)/shard_map/ppermute | solution.py:30
  47.6 16.7 %copy-start.11 = (bf16[128,2048]{1,0:T(8,128)(2,1)}, bf16[128,2048]{1,0:T(8,128)(2,1)S(1)}, u32[]{:S(2)}) copy-start(bf16[128,2048]{1,0:T(8,128)(2,1)S(1)} %collective-permute-done.16) | copy-start | bytes 1572868
  47.6 14.5 %collective-permute-start.17 = (bf16[128,2048]{1,0:T(8,128)(2,1)S(1)}, bf16[128,2048]{1,0:T(8,128)(2,1)S(1)}, u32[]{:S(2)}, u32[]{:S(2)}) collective-permute-start(bf16[128,2048]{1,0:T(8,128)(2,1)S(1)} %collective-permute-done.16), channel_id=1, source_target_pairs={{0,1},{1,2},{2,3},{3,4},{4,5},{5,6},{6,7},{7,8},{8,9},{9,10},{10,1... | collective-permute-start | bytes 1572872 | tf_op jit(solution)/shard_map/ppermute | solution.py:30
  50.3 13.7 %copy-start.6 = (f32[128,128]{1,0:T(8,128)}, f32[128,128]{1,0:T(8,128)S(1)}, u32[]{:S(2)}) copy-start(f32[128,128]{1,0:T(8,128)S(1)} %get-tuple-element.65) | copy-start | bytes 196612
  50.3 13.7 %copy-start.9 = (bf16[128,2048]{1,0:T(8,128)(2,1)}, bf16[128,2048]{1,0:T(8,128)(2,1)S(1)}, u32[]{:S(2)}) copy-start(bf16[128,2048]{1,0:T(8,128)(2,1)S(1)} %collective-permute-done.1) | copy-start | bytes 1572868
  50.3 14.0 %collective-permute-start.2 = (bf16[128,2048]{1,0:T(8,128)(2,1)S(1)}, bf16[128,2048]{1,0:T(8,128)(2,1)}, u32[]{:S(2)}, u32[]{:S(2)}) collective-permute-start(bf16[128,2048]{1,0:T(8,128)(2,1)S(1)} %collective-permute-done.1), channel_id=1, source_target_pairs={{0,31},{1,0},{2,1},{3,2},{4,3},{5,4},{6,5},{7,6},{8,7},{9,8},{10,9... | collective-permute-start | bytes 1572872 | tf_op jit(solution)/shard_map/ppermute | solution.py:30
  62.1 7.4 %copy-start.13 = (bf16[128,2048]{1,0:T(8,128)(2,1)}, bf16[128,2048]{1,0:T(8,128)(2,1)S(1)}, u32[]{:S(2)}) copy-start(bf16[128,2048]{1,0:T(8,128)(2,1)S(1)} %collective-permute-done.17) | copy-start | bytes 1572868
  62.1 13.7 %collective-permute-start.18 = (bf16[128,2048]{1,0:T(8,128)(2,1)S(1)}, bf16[128,2048]{1,0:T(8,128)(2,1)}, u32[]{:S(2)}, u32[]{:S(2)}) collective-permute-start(bf16[128,2048]{1,0:T(8,128)(2,1)S(1)} %collective-permute-done.17), channel_id=1, source_target_pairs={{0,1},{1,2},{2,3},{3,4},{4,5},{5,6},{6,7},{7,8},{8,9},{9,10},{10,1... | collective-permute-start | bytes 1572872 | tf_op jit(solution)/shard_map/ppermute | solution.py:30
  64.4 13.7 %collective-permute-start.3 = (bf16[128,2048]{1,0:T(8,128)(2,1)}, bf16[128,2048]{1,0:T(8,128)(2,1)}, u32[]{:S(2)}, u32[]{:S(2)}) collective-permute-start(bf16[128,2048]{1,0:T(8,128)(2,1)} %collective-permute-done.2), channel_id=1, source_target_pairs={{0,31},{1,0},{2,1},{3,2},{4,3},{5,4},{6,5},{7,6},{8,7},{9,8},{10,9... | collective-permute-start | bytes 1572872 | tf_op jit(solution)/shard_map/ppermute | solution.py:30
  75.8 13.1 %collective-permute-start.19 = (bf16[128,2048]{1,0:T(8,128)(2,1)}, bf16[128,2048]{1,0:T(8,128)(2,1)}, u32[]{:S(2)}, u32[]{:S(2)}) collective-permute-start(bf16[128,2048]{1,0:T(8,128)(2,1)} %collective-permute-done.18), channel_id=1, source_target_pairs={{0,1},{1,2},{2,3},{3,4},{4,5},{5,6},{6,7},{7,8},{8,9},{9,10},{10,1... | collective-permute-start | bytes 1572872 | tf_op jit(solution)/shard_map/ppermute | solution.py:30
  78.0 27.3 %collective-permute-start.4 = (bf16[128,2048]{1,0:T(8,128)(2,1)}, bf16[128,2048]{1,0:T(8,128)(2,1)}, u32[]{:S(2)}, u32[]{:S(2)}) collective-permute-start(bf16[128,2048]{1,0:T(8,128)(2,1)} %collective-permute-done.3), channel_id=1, source_target_pairs={{0,31},{1,0},{2,1},{3,2},{4,3},{5,4},{6,5},{7,6},{8,7},{9,8},{10,9... | collective-permute-start | bytes 1572872 | tf_op jit(solution)/shard_map/ppermute | solution.py:30
  88.9 20.8 %collective-permute-start.20 = (bf16[128,2048]{1,0:T(8,128)(2,1)}, bf16[128,2048]{1,0:T(8,128)(2,1)}, u32[]{:S(2)}, u32[]{:S(2)}) collective-permute-start(bf16[128,2048]{1,0:T(8,128)(2,1)} %collective-permute-done.19), channel_id=1, source_target_pairs={{0,1},{1,2},{2,3},{3,4},{4,5},{5,6},{6,7},{7,8},{8,9},{9,10},{10,1... | collective-permute-start | bytes 1572872 | tf_op jit(solution)/shard_map/ppermute | solution.py:30
  91.7 36.3 %all-to-all-start = ((f32[32,1,288]{2,1,0:T(1,128)}), f32[32,1,288]{2,1,0:T(1,128)}, u32[]{:S(2)}, u32[]{:S(2)}) async-start(f32[32,1,288]{2,1,0:T(1,128)} %copy.38), calls=%async_computation | async-start | bytes 98304 | tf_op jit(solution)/shard_map/all_to_all | solution.py:154
  105.3 25.4 %collective-permute-start.5 = (bf16[128,2048]{1,0:T(8,128)(2,1)}, bf16[128,2048]{1,0:T(8,128)(2,1)}, u32[]{:S(2)}, u32[]{:S(2)}) collective-permute-start(bf16[128,2048]{1,0:T(8,128)(2,1)} %collective-permute-done.4), channel_id=1, source_target_pairs={{0,31},{1,0},{2,1},{3,2},{4,3},{5,4},{6,5},{7,6},{8,7},{9,8},{10,9... | collective-permute-start | bytes 1572872 | tf_op jit(solution)/shard_map/ppermute | solution.py:30
  109.7 22.9 %collective-permute-start.21 = (bf16[128,2048]{1,0:T(8,128)(2,1)}, bf16[128,2048]{1,0:T(8,128)(2,1)}, u32[]{:S(2)}, u32[]{:S(2)}) collective-permute-start(bf16[128,2048]{1,0:T(8,128)(2,1)} %collective-permute-done.20), channel_id=1, source_target_pairs={{0,1},{1,2},{2,3},{3,4},{4,5},{5,6},{6,7},{7,8},{8,9},{9,10},{10,1... | collective-permute-start | bytes 1572872 | tf_op jit(solution)/shard_map/ppermute | solution.py:30
  130.7 5.3 %copy-start.4 = (f32[32,1,288]{0,2,1:T(8,128)}, f32[32,1,288]{0,2,1:T(8,128)S(1)}, u32[]{:S(2)}) copy-start(f32[32,1,288]{0,2,1:T(8,128)S(1)} %dynamic-slice_maximum_fusion) | copy-start | bytes 110596
  130.7 15.7 %collective-permute-start.6 = (bf16[128,2048]{1,0:T(8,128)(2,1)}, bf16[128,2048]{1,0:T(8,128)(2,1)}, u32[]{:S(2)}, u32[]{:S(2)}) collective-permute-start(bf16[128,2048]{1,0:T(8,128)(2,1)} %collective-permute-done.5), channel_id=1, source_target_pairs={{0,31},{1,0},{2,1},{3,2},{4,3},{5,4},{6,5},{7,6},{8,7},{9,8},{10,9... | collective-permute-start | bytes 1572872 | tf_op jit(solution)/shard_map/ppermute | solution.py:30
  132.6 16.9 %collective-permute-start.22 = (bf16[128,2048]{1,0:T(8,128)(2,1)}, bf16[128,2048]{1,0:T(8,128)(2,1)}, u32[]{:S(2)}, u32[]{:S(2)}) collective-permute-start(bf16[128,2048]{1,0:T(8,128)(2,1)} %collective-permute-done.21), channel_id=1, source_target_pairs={{0,1},{1,2},{2,3},{3,4},{4,5},{5,6},{6,7},{7,8},{8,9},{9,10},{10,1... | collective-permute-start | bytes 1572872 | tf_op jit(solution)/shard_map/ppermute | solution.py:30
  146.4 12.7 %collective-permute-start.7 = (bf16[128,2048]{1,0:T(8,128)(2,1)}, bf16[128,2048]{1,0:T(8,128)(2,1)S(1)}, u32[]{:S(2)}, u32[]{:S(2)}) collective-permute-start(bf16[128,2048]{1,0:T(8,128)(2,1)} %collective-permute-done.6), channel_id=1, source_target_pairs={{0,31},{1,0},{2,1},{3,2},{4,3},{5,4},{6,5},{7,6},{8,7},{9,8},{10,9... | collective-permute-start | bytes 1572872 | tf_op jit(solution)/shard_map/ppermute | solution.py:30
  159.5 32.3 %collective-permute-start.8 = (bf16[16,2048]{1,0:T(8,128)(2,1)S(1)}, bf16[16,2048]{1,0:T(8,128)(2,1)S(1)}, u32[]{:S(2)}, u32[]{:S(2)}) collective-permute-start(bf16[16,2048]{1,0:T(8,128)(2,1)S(1)} %get-tuple-element.43), channel_id=1, source_target_pairs={{0,31},{1,0},{2,1},{3,2},{4,3},{5,4},{6,5},{7,6},{8,7},{9,8},{10,9... | collective-permute-start | bytes 196616 | tf_op jit(solution)/shard_map/ppermute | solution.py:30
  175.8 21.5 %collective-permute-start.9 = (bf16[16,2048]{1,0:T(8,128)(2,1)S(1)}, bf16[16,2048]{1,0:T(8,128)(2,1)S(1)}, u32[]{:S(2)}, u32[]{:S(2)}) collective-permute-start(bf16[16,2048]{1,0:T(8,128)(2,1)S(1)} %get-tuple-element.42), channel_id=1, source_target_pairs={{0,30},{1,31},{2,0},{3,1},{4,2},{5,3},{6,4},{7,5},{8,6},{9,7},{10,... | collective-permute-start | bytes 196616 | tf_op jit(solution)/shard_map/ppermute | solution.py:30
  177.7 28.4 %collective-permute-start.10 = (bf16[16,2048]{1,0:T(8,128)(2,1)S(1)}, bf16[16,2048]{1,0:T(8,128)(2,1)S(1)}, u32[]{:S(2)}, u32[]{:S(2)}) collective-permute-start(bf16[16,2048]{1,0:T(8,128)(2,1)S(1)} %get-tuple-element.41), channel_id=1, source_target_pairs={{0,29},{1,30},{2,31},{3,0},{4,1},{5,2},{6,3},{7,4},{8,5},{9,6},{10... | collective-permute-start | bytes 196616 | tf_op jit(solution)/shard_map/ppermute | solution.py:30
  180.3 30.6 %collective-permute-start.11 = (bf16[16,2048]{1,0:T(8,128)(2,1)S(1)}, bf16[16,2048]{1,0:T(8,128)(2,1)S(1)}, u32[]{:S(2)}, u32[]{:S(2)}) collective-permute-start(bf16[16,2048]{1,0:T(8,128)(2,1)S(1)} %get-tuple-element.40), channel_id=1, source_target_pairs={{0,28},{1,29},{2,30},{3,31},{4,0},{5,1},{6,2},{7,3},{8,4},{9,5},{1... | collective-permute-start | bytes 196616 | tf_op jit(solution)/shard_map/ppermute | solution.py:30
  184.8 33.0 %collective-permute-start.12 = (bf16[16,2048]{1,0:T(8,128)(2,1)S(1)}, bf16[16,2048]{1,0:T(8,128)(2,1)S(1)}, u32[]{:S(2)}, u32[]{:S(2)}) collective-permute-start(bf16[16,2048]{1,0:T(8,128)(2,1)S(1)} %get-tuple-element.39), channel_id=1, source_target_pairs={{0,27},{1,28},{2,29},{3,30},{4,31},{5,0},{6,1},{7,2},{8,3},{9,4},{... | collective-permute-start | bytes 196616 | tf_op jit(solution)/shard_map/ppermute | solution.py:30
  191.9 29.6 %collective-permute-start.13 = (bf16[16,2048]{1,0:T(8,128)(2,1)S(1)}, bf16[16,2048]{1,0:T(8,128)(2,1)S(1)}, u32[]{:S(2)}, u32[]{:S(2)}) collective-permute-start(bf16[16,2048]{1,0:T(8,128)(2,1)S(1)} %get-tuple-element.38), channel_id=1, source_target_pairs={{0,26},{1,27},{2,28},{3,29},{4,30},{5,31},{6,0},{7,1},{8,2},{9,3},... | collective-permute-start | bytes 196616 | tf_op jit(solution)/shard_map/ppermute | solution.py:30
  197.3 31.1 %collective-permute-start.14 = (bf16[16,2048]{1,0:T(8,128)(2,1)S(1)}, bf16[16,2048]{1,0:T(8,128)(2,1)S(1)}, u32[]{:S(2)}, u32[]{:S(2)}) collective-permute-start(bf16[16,2048]{1,0:T(8,128)(2,1)S(1)} %get-tuple-element.37), channel_id=1, source_target_pairs={{0,25},{1,26},{2,27},{3,28},{4,29},{5,30},{6,31},{7,0},{8,1},{9,2}... | collective-permute-start | bytes 196616 | tf_op jit(solution)/shard_map/ppermute | solution.py:30
  206.1 26.8 %collective-permute-start.23 = (bf16[16,2048]{1,0:T(8,128)(2,1)S(1)}, bf16[16,2048]{1,0:T(8,128)(2,1)S(1)}, u32[]{:S(2)}, u32[]{:S(2)}) collective-permute-start(bf16[16,2048]{1,0:T(8,128)(2,1)S(1)} %get-tuple-element.36), channel_id=1, source_target_pairs={{0,8},{1,9},{2,10},{3,11},{4,12},{5,13},{6,14},{7,15},{8,16},{9,17... | collective-permute-start | bytes 196616 | tf_op jit(solution)/shard_map/ppermute | solution.py:39
  210.9 25.8 %collective-permute-start.24 = (bf16[16,2048]{1,0:T(8,128)(2,1)S(1)}, bf16[16,2048]{1,0:T(8,128)(2,1)S(1)}, u32[]{:S(2)}, u32[]{:S(2)}) collective-permute-start(bf16[16,2048]{1,0:T(8,128)(2,1)S(1)} %get-tuple-element.35), channel_id=1, source_target_pairs={{0,7},{1,8},{2,9},{3,10},{4,11},{5,12},{6,13},{7,14},{8,15},{9,16}... | collective-permute-start | bytes 196616 | tf_op jit(solution)/shard_map/ppermute | solution.py:30
  217.8 22.3 %collective-permute-start.25 = (bf16[16,2048]{1,0:T(8,128)(2,1)S(1)}, bf16[16,2048]{1,0:T(8,128)(2,1)S(1)}, u32[]{:S(2)}, u32[]{:S(2)}) collective-permute-start(bf16[16,2048]{1,0:T(8,128)(2,1)S(1)} %get-tuple-element.34), channel_id=1, source_target_pairs={{0,6},{1,7},{2,8},{3,9},{4,10},{5,11},{6,12},{7,13},{8,14},{9,15},... | collective-permute-start | bytes 196616 | tf_op jit(solution)/shard_map/ppermute | solution.py:30
  221.5 27.1 %collective-permute-start.26 = (bf16[16,2048]{1,0:T(8,128)(2,1)S(1)}, bf16[16,2048]{1,0:T(8,128)(2,1)S(1)}, u32[]{:S(2)}, u32[]{:S(2)}) collective-permute-start(bf16[16,2048]{1,0:T(8,128)(2,1)S(1)} %get-tuple-element.33), channel_id=1, source_target_pairs={{0,5},{1,6},{2,7},{3,8},{4,9},{5,10},{6,11},{7,12},{8,13},{9,14},{... | collective-permute-start | bytes 196616 | tf_op jit(solution)/shard_map/ppermute | solution.py:30
  228.3 25.1 %collective-permute-start.27 = (bf16[16,2048]{1,0:T(8,128)(2,1)S(1)}, bf16[16,2048]{1,0:T(8,128)(2,1)S(1)}, u32[]{:S(2)}, u32[]{:S(2)}) collective-permute-start(bf16[16,2048]{1,0:T(8,128)(2,1)S(1)} %get-tuple-element.32), channel_id=1, source_target_pairs={{0,4},{1,5},{2,6},{3,7},{4,8},{5,9},{6,10},{7,11},{8,12},{9,13},{1... | collective-permute-start | bytes 196616 | tf_op jit(solution)/shard_map/ppermute | solution.py:30
  232.9 28.6 %collective-permute-start.28 = (bf16[16,2048]{1,0:T(8,128)(2,1)S(1)}, bf16[16,2048]{1,0:T(8,128)(2,1)S(1)}, u32[]{:S(2)}, u32[]{:S(2)}) collective-permute-start(bf16[16,2048]{1,0:T(8,128)(2,1)S(1)} %get-tuple-element.31), channel_id=1, source_target_pairs={{0,3},{1,4},{2,5},{3,6},{4,7},{5,8},{6,9},{7,10},{8,11},{9,12},{10... | collective-permute-start | bytes 196616 | tf_op jit(solution)/shard_map/ppermute | solution.py:30
  236.7 25.0 %collective-permute-start.29 = (bf16[16,2048]{1,0:T(8,128)(2,1)S(1)}, bf16[16,2048]{1,0:T(8,128)(2,1)S(1)}, u32[]{:S(2)}, u32[]{:S(2)}) collective-permute-start(bf16[16,2048]{1,0:T(8,128)(2,1)S(1)} %get-tuple-element.30), channel_id=1, source_target_pairs={{0,2},{1,3},{2,4},{3,5},{4,6},{5,7},{6,8},{7,9},{8,10},{9,11},{10,... | collective-permute-start | bytes 196616 | tf_op jit(solution)/shard_map/ppermute | solution.py:30
  240.1 24.9 %collective-permute-start.30 = (bf16[16,2048]{1,0:T(8,128)(2,1)S(1)}, bf16[16,2048]{1,0:T(8,128)(2,1)S(1)}, u32[]{:S(2)}, u32[]{:S(2)}) collective-permute-start(bf16[16,2048]{1,0:T(8,128)(2,1)S(1)} %get-tuple-element.29), channel_id=1, source_target_pairs={{0,1},{1,2},{2,3},{3,4},{4,5},{5,6},{6,7},{7,8},{8,9},{9,10},{10,1... | collective-permute-start | bytes 196616 | tf_op jit(solution)/shard_map/ppermute | solution.py:30
  271.8 17.0 %copy-start.7 = (f32[128,128]{1,0:T(8,128)S(1)}, f32[128,128]{1,0:T(8,128)}, u32[]{:S(2)}) copy-start(f32[128,128]{1,0:T(8,128)} %copy-done.6) | copy-start | bytes 196612
  271.8 17.0 %copy-start.18 = (f32[128,128]{1,0:T(8,128)S(1)}, f32[128,128]{1,0:T(8,128)}, u32[]{:S(2)}) copy-start(f32[128,128]{1,0:T(8,128)} %get-tuple-element.66) | copy-start | bytes 196612
  271.8 17.0 %copy-start.20 = (pred[128,128]{1,0:T(8,128)(4,1)S(1)}, pred[128,128]{1,0:T(8,128)(4,1)}, u32[]{:S(2)}) copy-start(pred[128,128]{1,0:T(8,128)(4,1)} %get-tuple-element.68) | copy-start | bytes 49156
  271.8 17.0 %copy-start.21 = (pred[128,128]{1,0:T(8,128)(4,1)S(1)}, pred[128,128]{1,0:T(8,128)(4,1)}, u32[]{:S(2)}) copy-start(pred[128,128]{1,0:T(8,128)(4,1)} %get-tuple-element.69) | copy-start | bytes 49156
  271.8 17.0 %copy-start.22 = (pred[128,128]{1,0:T(8,128)(4,1)S(1)}, pred[128,128]{1,0:T(8,128)(4,1)}, u32[]{:S(2)}) copy-start(pred[128,128]{1,0:T(8,128)(4,1)} %get-tuple-element.70) | copy-start | bytes 49156
  271.8 17.0 %copy-start.23 = (pred[128,128]{1,0:T(8,128)(4,1)S(1)}, pred[128,128]{1,0:T(8,128)(4,1)}, u32[]{:S(2)}) copy-start(pred[128,128]{1,0:T(8,128)(4,1)} %get-tuple-element.71) | copy-start | bytes 49156
  271.8 17.0 %copy-start.24 = (pred[128,128]{1,0:T(8,128)(4,1)S(1)}, pred[128,128]{1,0:T(8,128)(4,1)}, u32[]{:S(2)}) copy-start(pred[128,128]{1,0:T(8,128)(4,1)} %get-tuple-element.72) | copy-start | bytes 49156
  271.9 17.0 %copy-start.30 = (f32[128]{0:T(128)S(1)}, f32[128]{0:T(128)}, u32[]{:S(2)}) copy-start(f32[128]{0:T(128)} %get-tuple-element.57) | copy-start | bytes 1540
  271.9 17.0 %copy-start.31 = (f32[128]{0:T(128)S(1)}, f32[128]{0:T(128)}, u32[]{:S(2)}) copy-start(f32[128]{0:T(128)} %get-tuple-element.61) | copy-start | bytes 1540
  271.9 17.0 %copy-start.32 = (f32[128]{0:T(128)S(1)}, f32[128]{0:T(128)}, u32[]{:S(2)}) copy-start(f32[128]{0:T(128)} %get-tuple-element.62) | copy-start | bytes 1540
  271.9 17.0 %copy-start.33 = (f32[128]{0:T(128)S(1)}, f32[128]{0:T(128)}, u32[]{:S(2)}) copy-start(f32[128]{0:T(128)} %get-tuple-element.63) | copy-start | bytes 1540
  271.9 17.0 %copy-start.34 = (f32[128]{0:T(128)S(1)}, f32[128]{0:T(128)}, u32[]{:S(2)}) copy-start(f32[128]{0:T(128)} %get-tuple-element.64) | copy-start | bytes 1540
  273.9 49.7 %collective-permute-start.31 = (bf16[16,24,2048]{2,1,0:T(8,128)(2,1)}, bf16[16,24,2048]{2,1,0:T(8,128)(2,1)}, u32[]{:S(2)}, u32[]{:S(2)}) collective-permute-start(bf16[16,24,2048]{2,1,0:T(8,128)(2,1)} %dynamic-slice_bitcast_fusion), channel_id=1, source_target_pairs={{0,32},{32,0},{64,96},{96,64},{128,160},{160,128},{192,224},{224,1... | collective-permute-start | bytes 4718600 | tf_op jit(solution)/shard_map/ppermute | solution.py:70
  277.2 32.8 %all-to-all-start.1 = ((f32[32,1,16]{2,1,0:T(1,128)}), f32[32,1,16]{2,1,0:T(1,128)S(1)}, u32[]{:S(2)}, u32[]{:S(2)}) async-start(f32[32,1,16]{2,1,0:T(1,128)} %bitcast.35), calls=%async_computation.1 | async-start | bytes 32768 | tf_op jit(solution)/shard_map/all_to_all | solution.py:187
  315.0 24.5 %all-to-all-start.2 = ((bf16[32,64,128]{2,1,0:T(8,128)(2,1)}), bf16[32,64,128]{2,1,0:T(8,128)(2,1)}, u32[]{:S(2)}, u32[]{:S(2)}) async-start(bf16[32,64,128]{2,1,0:T(8,128)(2,1)} %bitcast.186), calls=%async_computation.2 | async-start | bytes 1048576 | tf_op jit(solution)/shard_map/all_to_all | solution.py:19
  326.2 12.1 %copy-start.15 = (bf16[272,768]{1,0:T(8,128)(2,1)S(1)}, bf16[272,768]{1,0:T(8,128)(2,1)}, u32[]{:S(2)}) copy-start(bf16[272,768]{1,0:T(8,128)(2,1)} %get-tuple-element.25) | copy-start | bytes 1253380
  326.2 12.1 %copy-start.16 = (bf16[240,768]{1,0:T(8,128)(2,1)S(1)}, bf16[240,768]{1,0:T(8,128)(2,1)}, u32[]{:S(2)}) copy-start(bf16[240,768]{1,0:T(8,128)(2,1)} %get-tuple-element.27) | copy-start | bytes 1105924
  327.6 41.0 %collective-permute-start.32 = (bf16[4,24,2048]{2,1,0:T(8,128)(2,1)}, bf16[4,24,2048]{2,1,0:T(8,128)(2,1)}, u32[]{:S(2)}, u32[]{:S(2)}) collective-permute-start(bf16[4,24,2048]{2,1,0:T(8,128)(2,1)} %get-tuple-element.22), channel_id=1, source_target_pairs={{0,64},{32,96},{64,128},{96,160},{128,192},{160,224},{192,0},{224,... | collective-permute-start | bytes 1179656 | tf_op jit(solution)/shard_map/ppermute | solution.py:70
  330.8 37.7 %collective-permute-start.33 = (bf16[4,24,2048]{2,1,0:T(8,128)(2,1)}, bf16[4,24,2048]{2,1,0:T(8,128)(2,1)}, u32[]{:S(2)}, u32[]{:S(2)}) collective-permute-start(bf16[4,24,2048]{2,1,0:T(8,128)(2,1)} %get-tuple-element.24), channel_id=1, source_target_pairs={{0,128},{32,160},{64,192},{96,224},{128,0},{160,32},{192,64},{224,... | collective-permute-start | bytes 1179656 | tf_op jit(solution)/shard_map/ppermute | solution.py:70
  335.1 33.4 %collective-permute-start.34 = (bf16[4,24,2048]{2,1,0:T(8,128)(2,1)S(1)}, bf16[4,24,2048]{2,1,0:T(8,128)(2,1)}, u32[]{:S(2)}, u32[]{:S(2)}) collective-permute-start(bf16[4,24,2048]{2,1,0:T(8,128)(2,1)S(1)} %get-tuple-element.23), channel_id=1, source_target_pairs={{0,192},{32,224},{64,0},{96,32},{128,64},{160,96},{192,128},{224,1... | collective-permute-start | bytes 1179656 | tf_op jit(solution)/shard_map/ppermute | solution.py:70
  342.8 25.0 %all-to-all-start.3 = ((bf16[32,2,128]{2,1,0:T(2,128)(2,1)}), bf16[32,2,128]{2,1,0:T(2,128)(2,1)S(1)}, u32[]{:S(2)}, u32[]{:S(2)}) async-start(bf16[32,2,128]{2,1,0:T(2,128)(2,1)} %reshape.157), calls=%async_computation.3 | async-start | bytes 32768 | tf_op jit(solution)/shard_map/all_to_all | solution.py:19
  368.6 12.2 %copy-start.19 = (bf16[32,4,64]{2,1,0:T(4,128)(2,1)S(1)}, bf16[32,4,64]{2,1,0:T(4,128)(2,1)}, u32[]{:S(2)}) copy-start(bf16[32,4,64]{2,1,0:T(4,128)(2,1)} %reshape.158) | copy-start | bytes 49156
  370.2 11.2 %collective-permute-start.35 = (bf16[24,2048]{1,0:T(8,128)(2,1)S(1)}, bf16[24,2048]{1,0:T(8,128)(2,1)S(1)}, u32[]{:S(2)}, u32[]{:S(2)}) collective-permute-start(bf16[24,2048]{1,0:T(8,128)(2,1)S(1)} %get-tuple-element.44), channel_id=1, source_target_pairs={{0,256},{32,288},{64,320},{96,352},{128,384},{160,416},{192,448},{... | collective-permute-start | bytes 294920 | tf_op jit(solution)/shard_map/ppermute | solution.py:70
  373.3 8.1 %collective-permute-start.36 = (bf16[24,2048]{1,0:T(8,128)(2,1)S(1)}, bf16[24,2048]{1,0:T(8,128)(2,1)S(1)}, u32[]{:S(2)}, u32[]{:S(2)}) collective-permute-start(bf16[24,2048]{1,0:T(8,128)(2,1)S(1)} %get-tuple-element.46), channel_id=1, source_target_pairs={{0,512},{32,544},{64,576},{96,608},{128,640},{160,672},{192,704},{... | collective-permute-start | bytes 294920 | tf_op jit(solution)/shard_map/ppermute | solution.py:70
  377.7 5.9 %collective-permute-start.37 = (bf16[24,2048]{1,0:T(8,128)(2,1)S(1)}, bf16[24,2048]{1,0:T(8,128)(2,1)S(1)}, u32[]{:S(2)}, u32[]{:S(2)}) collective-permute-start(bf16[24,2048]{1,0:T(8,128)(2,1)S(1)} %get-tuple-element.45), channel_id=1, source_target_pairs={{0,768},{32,800},{64,832},{96,864},{128,896},{160,928},{192,960},{... | collective-permute-start | bytes 294920 | tf_op jit(solution)/shard_map/ppermute | solution.py:70
  (13 other events, 34.7 us)

commit v2 on v1

v2 whole, which is shorter than its diff:
```python
import jax
import jax.numpy as jnp
import numpy as np
from jax import lax
from jax.sharding import PartitionSpec as P


F32 = jnp.float32
BF16 = jnp.bfloat16
NEAR = 9
LANES = 128


def in_blocks(value, dim, peers):
    before, after = (value.shape[:dim], value.shape[dim + 1 :])
    return jnp.moveaxis(value.reshape(*before, peers, -1, *after), dim, 0)


def sum_at_owner(value, axis, dim):
    parts = in_blocks(value, dim, lax.axis_size(axis))
    arrived = lax.all_to_all(parts, axis, split_axis=0, concat_axis=0, tiled=True)
    return arrived.astype(F32).sum(axis=0)


def turned(value, start):
    twice = jnp.concatenate([value, value], axis=0)
    return lax.dynamic_slice_in_dim(twice, start, value.shape[0], axis=0)


def shift(value, step):
    n = lax.axis_size("expert")
    return lax.ppermute(value, "expert", [(k, (k + step) % n) for k in range(n)])


def tables(notes, peers, lanes, capacity):
    wanted = np.repeat(np.array(lanes), capacity)[:, None]
    lane = np.arange(LANES)[None]
    gates = row_products(jnp.asarray(lane == wanted, BF16), notes)
    slots = row_products(jnp.asarray(lane == wanted + peers, BF16), notes)
    at = lax.broadcasted_iota(jnp.int32, slots.shape, 0) % capacity
    return jnp.where(slots == at.astype(F32), gates, 0.0).astype(BF16)


def row_products(a, b):
    return lax.dot_general(a, b, (((1,), (1,)), ((), ())), preferred_element_type=F32)


def pick(table, block, width):
    return lax.dot_general(
        table, block[:, :width], (((1,), (0,)), ((), ())), preferred_element_type=F32
    ).astype(BF16)


def spread(rows, capacity, way):
    parts = {k + 1: [(0, r)] for k, r in enumerate(jnp.split(rows, rows.shape[0] // capacity))}
    step = 4
    while step:
        sent = [(k, far, r) for k in sorted(parts) if k >= step for far, r in parts[k]]
        parts = {k: v for k, v in parts.items() if k < step}
        got = shift(jnp.concatenate([r for _, _, r in sent], axis=0), way * step)
        for (k, far, _), r in zip(sent, jnp.split(got, len(sent))):
            parts.setdefault(k - step, []).append((far + step, r))
        step //= 2
    return [r for _, r in sorted(parts[0], key=lambda pair: pair[0])]


def through(rows, weight, hidden):
    raw = lax.dot_general(rows, weight, (((1,), (1,)), ((), ())), preferred_element_type=F32)
    return raw.astype(BF16), jnp.sum(raw * hidden.astype(F32), axis=1)


def across(hidden, rows):
    return lax.dot_general(hidden, rows, (((0,), (0,)), ((), ())), preferred_element_type=F32)


def shards(tokens_in, out_grad, expert_ids, rest_scores, router_weight, down_weight, saved_hidden):
    n = lax.axis_size("expert")
    me = lax.axis_index("expert")
    capacity = saved_hidden.shape[3]
    hidden_units = saved_hidden.shape[4]
    tokens, width = out_grad.shape
    scored = router_weight.shape[1]

    ids_t = expert_ids.T
    rest_t = rest_scores.T
    expert_at = lax.broadcasted_iota(jnp.int32, (scored, tokens), 0)
    logits = lax.dot_general(
        router_weight, tokens_in, (((0,), (1,)), ((), ())), preferred_element_type=F32
    )
    same = expert_at[None] == ids_t[:, None, :]
    chosen = jnp.any(same, axis=0)
    rest = jnp.sum(jnp.where(same, rest_t[:, None, :], 0.0), axis=0)
    highest = jnp.max(jnp.where(chosen, logits, -jnp.inf), axis=0, keepdims=True)
    power = jnp.where(chosen, jnp.exp(logits - highest), 0.0)
    gate = power / jnp.sum(power, axis=0, keepdims=True)
    hit = chosen[:n]
    earlier = lax.broadcasted_iota(jnp.int32, (tokens, tokens), 0) < lax.broadcasted_iota(
        jnp.int32, (tokens, tokens), 1
    )
    before = lax.dot_general(
        hit.astype(BF16), earlier.astype(BF16), (((1,), (0,)), ((), ())), preferred_element_type=F32
    )
    slot = jnp.where(hit, before, -1.0)
    gate_sent = gate[:n].astype(BF16).astype(F32)
    notes = turned(jnp.concatenate([gate_sent, slot], axis=1), me)
    notes = jnp.concatenate([notes[:, :tokens], notes[:, tokens:]], axis=0).T.astype(BF16)
    notes = jnp.pad(notes, ((0, 0), (0, LANES - 2 * n)))
    own = jnp.concatenate([out_grad, notes], axis=1)

    up, down = [own], [own]
    for _ in range(1, NEAR + 1):
        up.append(shift(up[-1], 1))
        down.append(shift(down[-1], -1))

    far_up = list(range(NEAR + 1, n // 2 + 1))
    far_down = [n - k for k in far_up[:-1]]
    up_rows = pick(tables(up[NEAR][:, width:], n, far_up, capacity), up[NEAR], width)
    low_rows = pick(tables(down[NEAR][:, width:], n, far_down, capacity), down[NEAR], width)
    top = spread(up_rows, capacity, 1)
    low = spread(low_rows, capacity, -1)

    blocks = [(h, up[h]) for h in range(NEAR, 0, -1)] + [(0, own)]
    blocks += [(n - h, down[h]) for h in range(1, NEAR + 1)]
    lane = lax.broadcasted_iota(jnp.int32, (tokens, LANES), 1) % n
    mixed = own[:, width:]
    for k, block in blocks:
        mixed = jnp.where(lane == k, block[:, width:], mixed)
    near_table = tables(mixed, n, [k for k, _ in blocks], capacity)
    near_rows = [
        pick(near_table[i * capacity : (i + 1) * capacity], block, width)
        for i, (_, block) in enumerate(blocks)
    ]
    near = jnp.concatenate(near_rows, axis=0)
    far = jnp.concatenate(low + top[::-1], axis=0)
    cut = near.shape[0]

    hidden = turned(saved_hidden[0, 0], (me + n - NEAR) % n).reshape(n * capacity, hidden_units)
    hid_near, score_near = through(near, down_weight[0], hidden[:cut])
    hid_far, score_far = through(far, down_weight[0], hidden[cut:])
    home = (NEAR + n - me) % n
    scores = jnp.concatenate([score_near, score_far], axis=0).reshape(n, 1, capacity)
    scores, far = lax.optimization_barrier((turned(scores, home), far))
    returned = lax.all_to_all(scores, "expert", split_axis=0, concat_axis=0, tiled=True)[:, 0]
    partial = (across(hidden[:cut], near) + across(hidden[cut:], far)).astype(BF16)
    down_grad = lax.psum_scatter(partial, "dp", scatter_dimension=0, tiled=True).astype(F32)
    hid_grad = jnp.concatenate([hid_near, hid_far], axis=0)
    hidden_grad = turned(hid_grad.reshape(n, capacity, hidden_units), home)

    placed = slot[:, None, :] == jnp.arange(capacity, dtype=F32)[None, :, None]
    there = jnp.sum(jnp.where(placed, returned[:, :, None], 0.0), axis=1)
    safe = jnp.where(gate_sent > 0.0, gate_sent, 1.0)
    there = jnp.where(gate_sent > 0.0, there * (gate[:n] / safe), 0.0)
    weighed = jnp.concatenate([there, (gate * rest)[n:]], axis=0)
    logit_grad = (weighed - gate * jnp.sum(weighed, axis=0, keepdims=True)).astype(BF16)
    share = lax.dot_general(
        tokens_in, logit_grad, (((0,), (1,)), ((), ())), preferred_element_type=F32
    ).astype(BF16)
    summed_rows = sum_at_owner(share, "dp", 0)
    router_grad = sum_at_owner(summed_rows.astype(BF16), "expert", 1)
    token_grad = lax.dot_general(
        logit_grad, router_weight, (((0,), (1,)), ((), ())), preferred_element_type=F32
    ).astype(BF16)
    return (token_grad, router_grad, down_grad[None], hidden_grad[None, None])


def solution(mesh):
    return jax.shard_map(
        shards,
        mesh=mesh,
        in_specs=(
            P(("dp", "expert"), None),
            P(("dp", "expert"), None),
            P(("dp", "expert"), None),
            P(("dp", "expert"), None),
            P(),
            P("expert", None, None),
            P("dp", "expert", None, None, None),
        ),
        out_specs=(
            P(("dp", "expert"), None),
            P("dp", "expert"),
            P("expert", "dp", None),
            P("dp", "expert", None, None, None),
        ),
        check_vma=False,
    )
```

time: 389 us -> 376 us (0.967)
  starting transfers between devices: 196 us -> 130 us
  waiting for transfers between devices: 112 us -> 163 us
  between operations: 2.03 us -> 15 us
  local copies, waits for them, and re-layouts: 22.3 us -> 15.3 us
    reduce_scatter x0 -> x1, waiting for transfers between devices: none -> 36.7 us  [shards(): lax.psum_scatter(partial, 'dp', scatter_dimension=0, tiled=True).astype(F32)]
    ppermute x30 -> x24, starting transfers between devices: 130 us -> 94.8 us  [shift(): lax.ppermute(value, 'expert', [(k, (k + step) % n) for k in range(n)])]
    ppermute x8 -> x0, starting transfers between devices: 29.2 us -> none  [the longest x7 24.4 us: from_peers(): got = lax.ppermute(out, 'dp', [(i, perm_of(i, step)) for i in range(place)])]
    ppermute x30 -> x24, waiting for transfers between devices: 55.7 us -> 76.8 us  [shift(): lax.ppermute(value, 'expert', [(k, (k + step) % n) for k in range(n)])]
    all_to_all x1 -> x0, waiting for transfers between devices: 14 us -> none  [shards(): lax.all_to_all(note, 'expert', split_axis=0, concat_axis=0, tiled=True)]
    all_to_all x1 -> x0, starting transfers between devices: 13.6 us -> none  [shards(): lax.all_to_all(note, 'expert', split_axis=0, concat_axis=0, tiled=True)]
    all_to_all x2, starting transfers between devices: 12.5 us -> 24.8 us  [sum_at_owner(): lax.all_to_all(parts, axis, split_axis=0, concat_axis=0, tiled=True)]
    all_to_all x2, waiting for transfers between devices: 19 us -> 27.9 us  [sum_at_owner(): lax.all_to_all(parts, axis, split_axis=0, concat_axis=0, tiled=True)]
  transfers between devices with their start and end apart: 42 -> 28, of which waited for: 15 -> 18; matrix products, arithmetic and copies ran while one was open for 16% -> 9% of each run, Pallas kernels for 0% -> 0%
where the time goes in v2:
time: 376 us; the launch traced here: 373 us
  waiting for transfers between devices  163 us (43%)
  starting transfers between devices  130 us (35%)
  matrix products  34.7 us (9%)
  other arithmetic  15.5 us (4%)
  local copies, waits for them, and re-layouts  15.3 us (4%)
  between operations  15 us (4%)
    ppermute x24, starting transfers between devices, shift(): lax.ppermute(value, 'expert', [(k, (k + step) % n) for k in range(n)])  94.8 us
    ppermute x24, waiting for transfers between devices, shift(): lax.ppermute(value, 'expert', [(k, (k + step) % n) for k in range(n)])  76.8 us
    reduce_scatter x1, waiting for transfers between devices, shards(): lax.psum_scatter(partial, 'dp', scatter_dimension=0, tiled=True).astype(F32)  36.7 us
    all_to_all x2, waiting for transfers between devices, sum_at_owner(): lax.all_to_all(parts, axis, split_axis=0, concat_axis=0, tiled=True)  27.9 us
    all_to_all x2, starting transfers between devices, sum_at_owner(): lax.all_to_all(parts, axis, split_axis=0, concat_axis=0, tiled=True)  24.8 us
    all_to_all x1, waiting for transfers between devices, shards(): lax.all_to_all(scores, 'expert', split_axis=0, concat_axis=0, tiled=True)  21.2 us
    dot_general x21, matrix products, pick(): lax.dot_general(table, block[:, :width], (((1,), (0,)), ((), ())), prefer...  15.7 us
    all_to_all x1, starting transfers between devices, shards(): lax.all_to_all(scores, 'expert', split_axis=0, concat_axis=0, tiled=True)  10.2 us
  transfers between devices with their start and end apart: 28, of which 18 were waited for; matrix products, arithmetic and copies ran while one was open for 9% of the time, Pallas kernels for 0%

profile of v2, /device:TPU:1, one launch (start us, length us, event | category | flops | bytes accessed | tf_op | source)
XLA Modules:
  0.0 372.8 jit_solution(1570310642367463059)
XLA Ops:
  8.3 1.6 select_reduce_fusion.2
  10.0 2.0 copy.26
  13.1 4.4 %collective-permute-start.9 = (bf16[128,2176]{0,1:T(8,128)(2,1)S(1)}, bf16[128,2176]{0,1:T(8,128)(2,1)S(1)}, u32[]{:S(2)}, u32[]{:S(2)}) collective-permute-start(bf16[128,2176]{0,1:T(8,128)(2,1)S(1)} %pad_maximum_fusion.1), channel_id=1, source_target_pairs={{0,1},{1,2},{2,3},{3,4},{4,5},{5,6},{6,7},{7,8},{8,9},{9,10},{10,1... | collective-permute-start | bytes 1671176 | tf_op jit(solution)/shard_map/ppermute | solution.py:32
  17.5 16.8 %collective-permute-start = (bf16[128,2176]{0,1:T(8,128)(2,1)S(1)}, bf16[128,2176]{0,1:T(8,128)(2,1)S(1)}, u32[]{:S(2)}, u32[]{:S(2)}) collective-permute-start(bf16[128,2176]{0,1:T(8,128)(2,1)S(1)} %pad_maximum_fusion.1), channel_id=1, source_target_pairs={{0,31},{1,0},{2,1},{3,2},{4,3},{5,4},{6,5},{7,6},{8,7},{9,8},{10,9... | collective-permute-start | bytes 1671176 | tf_op jit(solution)/shard_map/ppermute | solution.py:32
  34.3 10.4 %collective-permute-done.9 = bf16[128,2176]{0,1:T(8,128)(2,1)S(1)} collective-permute-done((bf16[128,2176]{0,1:T(8,128)(2,1)S(1)}, bf16[128,2176]{0,1:T(8,128)(2,1)S(1)}, u32[]{:S(2)}, u32[]{:S(2)}) %collective-permute-start.9) | collective-permute-done | bytes 557088 | tf_op jit(solution)/shard_map/ppermute | solution.py:32
  44.7 1.9 collective-permute-start.10
  47.4 4.6 %collective-permute-start.1 = (bf16[128,2176]{0,1:T(8,128)(2,1)S(1)}, bf16[128,2176]{0,1:T(8,128)(2,1)S(1)}, u32[]{:S(2)}, u32[]{:S(2)}) collective-permute-start(bf16[128,2176]{0,1:T(8,128)(2,1)S(1)} %collective-permute-done), channel_id=1, source_target_pairs={{0,31},{1,0},{2,1},{3,2},{4,3},{5,4},{6,5},{7,6},{8,7},{9,8},{10,9... | collective-permute-start | bytes 1671176 | tf_op jit(solution)/shard_map/ppermute | solution.py:32
  52.0 8.7 %collective-permute-done.10 = bf16[128,2176]{0,1:T(8,128)(2,1)S(1)} collective-permute-done((bf16[128,2176]{0,1:T(8,128)(2,1)S(1)}, bf16[128,2176]{0,1:T(8,128)(2,1)S(1)}, u32[]{:S(2)}, u32[]{:S(2)}) %collective-permute-start.10) | collective-permute-done | bytes 557088 | tf_op jit(solution)/shard_map/ppermute | solution.py:32
  60.7 1.9 collective-permute-start.11
  62.7 5.1 %collective-permute-start.2 = (bf16[128,2176]{0,1:T(8,128)(2,1)S(1)}, bf16[128,2176]{0,1:T(8,128)(2,1)S(1)}, u32[]{:S(2)}, u32[]{:S(2)}) collective-permute-start(bf16[128,2176]{0,1:T(8,128)(2,1)S(1)} %collective-permute-done.1), channel_id=1, source_target_pairs={{0,31},{1,0},{2,1},{3,2},{4,3},{5,4},{6,5},{7,6},{8,7},{9,8},{10,9... | collective-permute-start | bytes 1671176 | tf_op jit(solution)/shard_map/ppermute | solution.py:32
  67.8 8.1 %collective-permute-done.11 = bf16[128,2176]{0,1:T(8,128)(2,1)S(1)} collective-permute-done((bf16[128,2176]{0,1:T(8,128)(2,1)S(1)}, bf16[128,2176]{0,1:T(8,128)(2,1)S(1)}, u32[]{:S(2)}, u32[]{:S(2)}) %collective-permute-start.11) | collective-permute-done | bytes 557088 | tf_op jit(solution)/shard_map/ppermute | solution.py:32
  75.9 1.9 collective-permute-start.12
  77.8 4.8 %collective-permute-start.3 = (bf16[128,2176]{0,1:T(8,128)(2,1)S(1)}, bf16[128,2176]{0,1:T(8,128)(2,1)S(1)}, u32[]{:S(2)}, u32[]{:S(2)}) collective-permute-start(bf16[128,2176]{0,1:T(8,128)(2,1)S(1)} %collective-permute-done.2), channel_id=1, source_target_pairs={{0,31},{1,0},{2,1},{3,2},{4,3},{5,4},{6,5},{7,6},{8,7},{9,8},{10,9... | collective-permute-start | bytes 1671176 | tf_op jit(solution)/shard_map/ppermute | solution.py:32
  82.6 7.5 %collective-permute-done.12 = bf16[128,2176]{0,1:T(8,128)(2,1)S(1)} collective-permute-done((bf16[128,2176]{0,1:T(8,128)(2,1)S(1)}, bf16[128,2176]{0,1:T(8,128)(2,1)S(1)}, u32[]{:S(2)}, u32[]{:S(2)}) %collective-permute-start.12) | collective-permute-done | bytes 557088 | tf_op jit(solution)/shard_map/ppermute | solution.py:32
  90.2 1.9 collective-permute-start.13
  92.9 4.6 %collective-permute-start.4 = (bf16[128,2176]{0,1:T(8,128)(2,1)S(1)}, bf16[128,2176]{0,1:T(8,128)(2,1)S(1)}, u32[]{:S(2)}, u32[]{:S(2)}) collective-permute-start(bf16[128,2176]{0,1:T(8,128)(2,1)S(1)} %collective-permute-done.3), channel_id=1, source_target_pairs={{0,31},{1,0},{2,1},{3,2},{4,3},{5,4},{6,5},{7,6},{8,7},{9,8},{10,9... | collective-permute-start | bytes 1671176 | tf_op jit(solution)/shard_map/ppermute | solution.py:32
  97.5 6.2 %collective-permute-done.13 = bf16[128,2176]{0,1:T(8,128)(2,1)S(1)} collective-permute-done((bf16[128,2176]{0,1:T(8,128)(2,1)S(1)}, bf16[128,2176]{0,1:T(8,128)(2,1)S(1)}, u32[]{:S(2)}, u32[]{:S(2)}) %collective-permute-start.13) | collective-permute-done | bytes 557088 | tf_op jit(solution)/shard_map/ppermute | solution.py:32
  103.7 1.9 collective-permute-start.14
  105.6 5.1 %collective-permute-start.5 = (bf16[128,2176]{0,1:T(8,128)(2,1)S(1)}, bf16[128,2176]{0,1:T(8,128)(2,1)}, u32[]{:S(2)}, u32[]{:S(2)}) collective-permute-start(bf16[128,2176]{0,1:T(8,128)(2,1)S(1)} %collective-permute-done.4), channel_id=1, source_target_pairs={{0,31},{1,0},{2,1},{3,2},{4,3},{5,4},{6,5},{7,6},{8,7},{9,8},{10,9... | collective-permute-start | bytes 1671176 | tf_op jit(solution)/shard_map/ppermute | solution.py:32
  110.7 5.6 %collective-permute-done.14 = bf16[128,2176]{0,1:T(8,128)(2,1)S(1)} collective-permute-done((bf16[128,2176]{0,1:T(8,128)(2,1)S(1)}, bf16[128,2176]{0,1:T(8,128)(2,1)S(1)}, u32[]{:S(2)}, u32[]{:S(2)}) %collective-permute-start.14) | collective-permute-done | bytes 557088 | tf_op jit(solution)/shard_map/ppermute | solution.py:32
  116.3 1.9 collective-permute-start.15
  118.2 4.9 %collective-permute-start.6 = (bf16[128,2176]{0,1:T(8,128)(2,1)}, bf16[128,2176]{0,1:T(8,128)(2,1)}, u32[]{:S(2)}, u32[]{:S(2)}) collective-permute-start(bf16[128,2176]{0,1:T(8,128)(2,1)} %collective-permute-done.5), channel_id=1, source_target_pairs={{0,31},{1,0},{2,1},{3,2},{4,3},{5,4},{6,5},{7,6},{8,7},{9,8},{10,9... | collective-permute-start | bytes 1671176 | tf_op jit(solution)/shard_map/ppermute | solution.py:32
  123.1 4.7 %collective-permute-done.15 = bf16[128,2176]{0,1:T(8,128)(2,1)} collective-permute-done((bf16[128,2176]{0,1:T(8,128)(2,1)S(1)}, bf16[128,2176]{0,1:T(8,128)(2,1)}, u32[]{:S(2)}, u32[]{:S(2)}) %collective-permute-start.15) | collective-permute-done | bytes 557088 | tf_op jit(solution)/shard_map/ppermute | solution.py:32
  127.9 1.9 collective-permute-start.16
  129.8 1.5 fusion.32
  133.8 4.6 %collective-permute-start.7 = (bf16[128,2176]{0,1:T(8,128)(2,1)}, bf16[128,2176]{0,1:T(8,128)(2,1)}, u32[]{:S(2)}, u32[]{:S(2)}) collective-permute-start(bf16[128,2176]{0,1:T(8,128)(2,1)} %collective-permute-done.6), channel_id=1, source_target_pairs={{0,31},{1,0},{2,1},{3,2},{4,3},{5,4},{6,5},{7,6},{8,7},{9,8},{10,9... | collective-permute-start | bytes 1671176 | tf_op jit(solution)/shard_map/ppermute | solution.py:32
  138.4 1.4 collective-permute-done.16
  139.8 1.9 collective-permute-start.17
  145.2 5.0 %collective-permute-start.8 = (bf16[128,2176]{0,1:T(8,128)(2,1)}, bf16[128,2176]{0,1:T(8,128)(2,1)}, u32[]{:S(2)}, u32[]{:S(2)}) collective-permute-start(bf16[128,2176]{0,1:T(8,128)(2,1)} %collective-permute-done.7), channel_id=1, source_target_pairs={{0,31},{1,0},{2,1},{3,2},{4,3},{5,4},{6,5},{7,6},{8,7},{9,8},{10,9... | collective-permute-start | bytes 1671176 | tf_op jit(solution)/shard_map/ppermute | solution.py:32
  150.2 2.6 collective-permute-done.17
  153.6 1.5 fusion.88
  155.1 2.3 convolution_convert_fusion.2
  157.5 1.7 split.132
  159.1 1.6 fusion.134
  160.7 1.5 fusion.92
  162.2 2.3 convolution_convert_fusion.3
  168.5 1.4 fusion.22
  169.8 1.4 fusion.21
  173.1 2.0 collective-permute-start.21
  175.1 7.3 %collective-permute-start.18 = (bf16[48,2048]{1,0:T(8,128)(2,1)S(1)}, bf16[48,2048]{1,0:T(8,128)(2,1)S(1)}, u32[]{:S(2)}, u32[]{:S(2)}) collective-permute-start(bf16[48,2048]{1,0:T(8,128)(2,1)S(1)} %split.119), channel_id=1, source_target_pairs={{0,28},{1,29},{2,30},{3,31},{4,0},{5,1},{6,2},{7,3},{8,4},{9,5},{1... | collective-permute-start | bytes 589832 | tf_op jit(solution)/shard_map/ppermute | solution.py:32
  183.7 1.3 fusion.8
  186.3 1.3 fusion.6
  187.6 1.3 fusion.5
  189.0 3.1 collective-permute-start.19
  193.4 1.9 collective-permute-start.22
  195.4 2.0 fusion.132
  197.3 6.0 %collective-permute-done.19 = bf16[48,2048]{1,0:T(8,128)(2,1)S(1)} collective-permute-done((bf16[48,2048]{1,0:T(8,128)(2,1)S(1)}, bf16[48,2048]{1,0:T(8,128)(2,1)S(1)}, u32[]{:S(2)}, u32[]{:S(2)}) %collective-permute-start.19) | collective-permute-done | bytes 196640 | tf_op jit(solution)/shard_map/ppermute | solution.py:32
  203.4 3.3 collective-permute-start.20
  206.8 2.1 collective-permute-start.23
  210.2 11.9 %collective-permute-done.23 = bf16[64,2048]{1,0:T(8,128)(2,1)S(1)} collective-permute-done((bf16[64,2048]{1,0:T(8,128)(2,1)S(1)}, bf16[64,2048]{1,0:T(8,128)(2,1)S(1)}, u32[]{:S(2)}, u32[]{:S(2)}) %collective-permute-start.23) | collective-permute-done | bytes 262176 | tf_op jit(solution)/shard_map/ppermute | solution.py:32
  222.2 1.9 fusion.133
  224.9 2.3 fusion.140
  227.2 3.5 add_convert_fusion
  231.4 10.2 %all-to-all-start = ((f32[32,1,16]{2,1,0:T(1,128)}), f32[32,1,16]{2,1,0:T(1,128)S(1)}, u32[]{:S(2)}, u32[]{:S(2)}) async-start(f32[32,1,16]{2,1,0:T(1,128)} %bitcast.6), calls=%async_computation | async-start | bytes 32768 | tf_op jit(solution)/shard_map/all_to_all | solution.py:143
  241.7 21.2 %all-to-all-done = f32[32,1,16]{2,1,0:T(1,128)S(1)} async-done(((f32[32,1,16]{2,1,0:T(1,128)}), f32[32,1,16]{2,1,0:T(1,128)S(1)}, u32[]{:S(2)}, u32[]{:S(2)}) %all-to-all-start) | async-done | bytes 2080 | tf_op jit(solution)/shard_map/all_to_all | solution.py:143
  263.7 2.1 fusion.4
  265.8 2.1 copy.28
  267.9 21.0 %all-to-all-start.1 = ((bf16[32,64,128]{2,1,0:T(8,128)(2,1)}), bf16[32,64,128]{2,1,0:T(8,128)(2,1)}, u32[]{:S(2)}, u32[]{:S(2)}) async-start(bf16[32,64,128]{2,1,0:T(8,128)(2,1)} %bitcast.55), calls=%async_computation.1 | async-start | bytes 1048576 | tf_op jit(solution)/shard_map/all_to_all | solution.py:21
  291.2 9.2 %all-to-all-done.1 = bf16[32,64,128]{2,1,0:T(8,128)(2,1)} async-done(((bf16[32,64,128]{2,1,0:T(8,128)(2,1)}), bf16[32,64,128]{2,1,0:T(8,128)(2,1)}, u32[]{:S(2)}, u32[]{:S(2)}) %all-to-all-start.1) | async-done | bytes 524320 | tf_op jit(solution)/shard_map/all_to_all | solution.py:21
  302.3 3.8 %all-to-all-start.2 = ((bf16[32,2,128]{2,1,0:T(2,128)(2,1)}), bf16[32,2,128]{2,1,0:T(2,128)(2,1)S(1)}, u32[]{:S(2)}, u32[]{:S(2)}) async-start(bf16[32,2,128]{2,1,0:T(2,128)(2,1)} %reshape.39), calls=%async_computation.2 | async-start | bytes 32768 | tf_op jit(solution)/shard_map/all_to_all | solution.py:21
  306.1 2.2 convolution_convert_fusion.1
  308.3 18.7 %all-to-all-done.2 = bf16[32,2,128]{2,1,0:T(2,128)(2,1)S(1)} async-done(((bf16[32,2,128]{2,1,0:T(2,128)(2,1)}), bf16[32,2,128]{2,1,0:T(2,128)(2,1)S(1)}, u32[]{:S(2)}, u32[]{:S(2)}) %all-to-all-start.2) | async-done | bytes 16416 | tf_op jit(solution)/shard_map/all_to_all | solution.py:21
  327.7 36.7 %reduce-scatter.2.cloned.1.call-done = bf16[24,2048]{1,0:T(8,128)(2,1)} async-done(((bf16[768,2048]{1,0:T(8,128)(2,1)}), bf16[24,2048]{1,0:T(8,128)(2,1)}) %reduce-scatter.2.cloned.1.call-update) | async-done | bytes 98320 | tf_op jit(solution)/shard_map/reduce_scatter | solution.py:145
  364.4 1.6 bitcast_convert_fusion
  (181 shorter events, 28.9 us)
Async XLA Ops:
  7.2 188.2 %copy-start = (bf16[1,768,2048]{2,1,0:T(8,128)(2,1)S(1)}, bf16[1,768,2048]{2,1,0:T(8,128)(2,1)}, u32[]{:S(2)}) copy-start(bf16[1,768,2048]{2,1,0:T(8,128)(2,1)} %param.18) | copy-start | bytes 9437188
  7.2 357.2 %reduce-scatter.2.cloned.1.call-start = ((), (), s32[]{:S(2)}) async-start(), calls=%async_computation.4 | async-start | bytes 3244032 | tf_op jit(solution)/shard_map/reduce_scatter | solution.py:145
  8.3 3.8 %copy-start.39 = (f32[32,128]{1,0:T(8,128)}, f32[32,128]{1,0:T(8,128)S(1)}, u32[]{:S(2)}) copy-start(f32[32,128]{1,0:T(8,128)S(1)} %convolution_select_fusion) | copy-start | bytes 49156
  13.1 31.5 %collective-permute-start.9 = (bf16[128,2176]{0,1:T(8,128)(2,1)S(1)}, bf16[128,2176]{0,1:T(8,128)(2,1)S(1)}, u32[]{:S(2)}, u32[]{:S(2)}) collective-permute-start(bf16[128,2176]{0,1:T(8,128)(2,1)S(1)} %pad_maximum_fusion.1), channel_id=1, source_target_pairs={{0,1},{1,2},{2,3},{3,4},{4,5},{5,6},{6,7},{7,8},{8,9},{9,10},{10,1... | collective-permute-start | bytes 1671176 | tf_op jit(solution)/shard_map/ppermute | solution.py:32
  17.5 29.1 %collective-permute-start = (bf16[128,2176]{0,1:T(8,128)(2,1)S(1)}, bf16[128,2176]{0,1:T(8,128)(2,1)S(1)}, u32[]{:S(2)}, u32[]{:S(2)}) collective-permute-start(bf16[128,2176]{0,1:T(8,128)(2,1)S(1)} %pad_maximum_fusion.1), channel_id=1, source_target_pairs={{0,31},{1,0},{2,1},{3,2},{4,3},{5,4},{6,5},{7,6},{8,7},{9,8},{10,9... | collective-permute-start | bytes 1671176 | tf_op jit(solution)/shard_map/ppermute | solution.py:32
  44.7 18.0 %copy-start.11 = (bf16[128,2176]{0,1:T(8,128)(2,1)}, bf16[128,2176]{0,1:T(8,128)(2,1)S(1)}, u32[]{:S(2)}) copy-start(bf16[128,2176]{0,1:T(8,128)(2,1)S(1)} %collective-permute-done.9) | copy-start | bytes 1671172
  44.7 16.0 %collective-permute-start.10 = (bf16[128,2176]{0,1:T(8,128)(2,1)S(1)}, bf16[128,2176]{0,1:T(8,128)(2,1)S(1)}, u32[]{:S(2)}, u32[]{:S(2)}) collective-permute-start(bf16[128,2176]{0,1:T(8,128)(2,1)S(1)} %collective-permute-done.9), channel_id=1, source_target_pairs={{0,1},{1,2},{2,3},{3,4},{4,5},{5,6},{6,7},{7,8},{8,9},{9,10},{10,1... | collective-permute-start | bytes 1671176 | tf_op jit(solution)/shard_map/ppermute | solution.py:32
  47.4 15.2 %collective-permute-start.1 = (bf16[128,2176]{0,1:T(8,128)(2,1)S(1)}, bf16[128,2176]{0,1:T(8,128)(2,1)S(1)}, u32[]{:S(2)}, u32[]{:S(2)}) collective-permute-start(bf16[128,2176]{0,1:T(8,128)(2,1)S(1)} %collective-permute-done), channel_id=1, source_target_pairs={{0,31},{1,0},{2,1},{3,2},{4,3},{5,4},{6,5},{7,6},{8,7},{9,8},{10,9... | collective-permute-start | bytes 1671176 | tf_op jit(solution)/shard_map/ppermute | solution.py:32
  60.7 17.1 %copy-start.15 = (bf16[128,2176]{0,1:T(8,128)(2,1)}, bf16[128,2176]{0,1:T(8,128)(2,1)S(1)}, u32[]{:S(2)}) copy-start(bf16[128,2176]{0,1:T(8,128)(2,1)S(1)} %collective-permute-done.10) | copy-start | bytes 1671172
  60.7 15.2 %collective-permute-start.11 = (bf16[128,2176]{0,1:T(8,128)(2,1)S(1)}, bf16[128,2176]{0,1:T(8,128)(2,1)S(1)}, u32[]{:S(2)}, u32[]{:S(2)}) collective-permute-start(bf16[128,2176]{0,1:T(8,128)(2,1)S(1)} %collective-permute-done.10), channel_id=1, source_target_pairs={{0,1},{1,2},{2,3},{3,4},{4,5},{5,6},{6,7},{7,8},{8,9},{9,10},{10,1... | collective-permute-start | bytes 1671176 | tf_op jit(solution)/shard_map/ppermute | solution.py:32
  62.6 5.1 %copy-start.13 = (bf16[128,2176]{0,1:T(8,128)(2,1)}, bf16[128,2176]{0,1:T(8,128)(2,1)S(1)}, u32[]{:S(2)}) copy-start(bf16[128,2176]{0,1:T(8,128)(2,1)S(1)} %collective-permute-done.1) | copy-start | bytes 1671172
  62.7 15.1 %collective-permute-start.2 = (bf16[128,2176]{0,1:T(8,128)(2,1)S(1)}, bf16[128,2176]{0,1:T(8,128)(2,1)S(1)}, u32[]{:S(2)}, u32[]{:S(2)}) collective-permute-start(bf16[128,2176]{0,1:T(8,128)(2,1)S(1)} %collective-permute-done.1), channel_id=1, source_target_pairs={{0,31},{1,0},{2,1},{3,2},{4,3},{5,4},{6,5},{7,6},{8,7},{9,8},{10,9... | collective-permute-start | bytes 1671176 | tf_op jit(solution)/shard_map/ppermute | solution.py:32
  75.9 29.7 %copy-start.21 = (bf16[128,2176]{0,1:T(8,128)(2,1)}, bf16[128,2176]{0,1:T(8,128)(2,1)S(1)}, u32[]{:S(2)}) copy-start(bf16[128,2176]{0,1:T(8,128)(2,1)S(1)} %collective-permute-done.11) | copy-start | bytes 1671172
  75.9 14.3 %collective-permute-start.12 = (bf16[128,2176]{0,1:T(8,128)(2,1)S(1)}, bf16[128,2176]{0,1:T(8,128)(2,1)S(1)}, u32[]{:S(2)}, u32[]{:S(2)}) collective-permute-start(bf16[128,2176]{0,1:T(8,128)(2,1)S(1)} %collective-permute-done.11), channel_id=1, source_target_pairs={{0,1},{1,2},{2,3},{3,4},{4,5},{5,6},{6,7},{7,8},{8,9},{9,10},{10,1... | collective-permute-start | bytes 1671176 | tf_op jit(solution)/shard_map/ppermute | solution.py:32
  77.8 4.8 %copy-start.17 = (bf16[128,2176]{0,1:T(8,128)(2,1)}, bf16[128,2176]{0,1:T(8,128)(2,1)S(1)}, u32[]{:S(2)}) copy-start(bf16[128,2176]{0,1:T(8,128)(2,1)S(1)} %collective-permute-done.2) | copy-start | bytes 1671172
  77.8 14.3 %collective-permute-start.3 = (bf16[128,2176]{0,1:T(8,128)(2,1)S(1)}, bf16[128,2176]{0,1:T(8,128)(2,1)S(1)}, u32[]{:S(2)}, u32[]{:S(2)}) collective-permute-start(bf16[128,2176]{0,1:T(8,128)(2,1)S(1)} %collective-permute-done.2), channel_id=1, source_target_pairs={{0,31},{1,0},{2,1},{3,2},{4,3},{5,4},{6,5},{7,6},{8,7},{9,8},{10,9... | collective-permute-start | bytes 1671176 | tf_op jit(solution)/shard_map/ppermute | solution.py:32
  90.2 28.0 %copy-start.25 = (bf16[128,2176]{0,1:T(8,128)(2,1)}, bf16[128,2176]{0,1:T(8,128)(2,1)S(1)}, u32[]{:S(2)}) copy-start(bf16[128,2176]{0,1:T(8,128)(2,1)S(1)} %collective-permute-done.12) | copy-start | bytes 1671172
  90.2 13.5 %collective-permute-start.13 = (bf16[128,2176]{0,1:T(8,128)(2,1)S(1)}, bf16[128,2176]{0,1:T(8,128)(2,1)S(1)}, u32[]{:S(2)}, u32[]{:S(2)}) collective-permute-start(bf16[128,2176]{0,1:T(8,128)(2,1)S(1)} %collective-permute-done.12), channel_id=1, source_target_pairs={{0,1},{1,2},{2,3},{3,4},{4,5},{5,6},{6,7},{7,8},{8,9},{9,10},{10,1... | collective-permute-start | bytes 1671176 | tf_op jit(solution)/shard_map/ppermute | solution.py:32
  92.9 12.7 %collective-permute-start.4 = (bf16[128,2176]{0,1:T(8,128)(2,1)S(1)}, bf16[128,2176]{0,1:T(8,128)(2,1)S(1)}, u32[]{:S(2)}, u32[]{:S(2)}) collective-permute-start(bf16[128,2176]{0,1:T(8,128)(2,1)S(1)} %collective-permute-done.3), channel_id=1, source_target_pairs={{0,31},{1,0},{2,1},{3,2},{4,3},{5,4},{6,5},{7,6},{8,7},{9,8},{10,9... | collective-permute-start | bytes 1671176 | tf_op jit(solution)/shard_map/ppermute | solution.py:32
  103.7 19.5 %copy-start.27 = (bf16[128,2176]{0,1:T(8,128)(2,1)}, bf16[128,2176]{0,1:T(8,128)(2,1)S(1)}, u32[]{:S(2)}) copy-start(bf16[128,2176]{0,1:T(8,128)(2,1)S(1)} %collective-permute-done.13) | copy-start | bytes 1671172
  103.7 12.6 %collective-permute-start.14 = (bf16[128,2176]{0,1:T(8,128)(2,1)S(1)}, bf16[128,2176]{0,1:T(8,128)(2,1)S(1)}, u32[]{:S(2)}, u32[]{:S(2)}) collective-permute-start(bf16[128,2176]{0,1:T(8,128)(2,1)S(1)} %collective-permute-done.13), channel_id=1, source_target_pairs={{0,1},{1,2},{2,3},{3,4},{4,5},{5,6},{6,7},{7,8},{8,9},{9,10},{10,1... | collective-permute-start | bytes 1671176 | tf_op jit(solution)/shard_map/ppermute | solution.py:32
  105.6 5.1 %copy-start.23 = (bf16[128,2176]{0,1:T(8,128)(2,1)}, bf16[128,2176]{0,1:T(8,128)(2,1)S(1)}, u32[]{:S(2)}) copy-start(bf16[128,2176]{0,1:T(8,128)(2,1)S(1)} %collective-permute-done.4) | copy-start | bytes 1671172
  105.6 12.6 %collective-permute-start.5 = (bf16[128,2176]{0,1:T(8,128)(2,1)S(1)}, bf16[128,2176]{0,1:T(8,128)(2,1)}, u32[]{:S(2)}, u32[]{:S(2)}) collective-permute-start(bf16[128,2176]{0,1:T(8,128)(2,1)S(1)} %collective-permute-done.4), channel_id=1, source_target_pairs={{0,31},{1,0},{2,1},{3,2},{4,3},{5,4},{6,5},{7,6},{8,7},{9,8},{10,9... | collective-permute-start | bytes 1671176 | tf_op jit(solution)/shard_map/ppermute | solution.py:32
  116.3 11.6 %copy-start.29 = (bf16[128,2176]{0,1:T(8,128)(2,1)}, bf16[128,2176]{0,1:T(8,128)(2,1)S(1)}, u32[]{:S(2)}) copy-start(bf16[128,2176]{0,1:T(8,128)(2,1)S(1)} %collective-permute-done.14) | copy-start | bytes 1671172
  116.3 11.6 %collective-permute-start.15 = (bf16[128,2176]{0,1:T(8,128)(2,1)S(1)}, bf16[128,2176]{0,1:T(8,128)(2,1)}, u32[]{:S(2)}, u32[]{:S(2)}) collective-permute-start(bf16[128,2176]{0,1:T(8,128)(2,1)S(1)} %collective-permute-done.14), channel_id=1, source_target_pairs={{0,1},{1,2},{2,3},{3,4},{4,5},{5,6},{6,7},{7,8},{8,9},{9,10},{10,1... | collective-permute-start | bytes 1671176 | tf_op jit(solution)/shard_map/ppermute | solution.py:32
  118.2 15.6 %collective-permute-start.6 = (bf16[128,2176]{0,1:T(8,128)(2,1)}, bf16[128,2176]{0,1:T(8,128)(2,1)}, u32[]{:S(2)}, u32[]{:S(2)}) collective-permute-start(bf16[128,2176]{0,1:T(8,128)(2,1)} %collective-permute-done.5), channel_id=1, source_target_pairs={{0,31},{1,0},{2,1},{3,2},{4,3},{5,4},{6,5},{7,6},{8,7},{9,8},{10,9... | collective-permute-start | bytes 1671176 | tf_op jit(solution)/shard_map/ppermute | solution.py:32
  127.9 12.0 %collective-permute-start.16 = (bf16[128,2176]{0,1:T(8,128)(2,1)}, bf16[128,2176]{0,1:T(8,128)(2,1)}, u32[]{:S(2)}, u32[]{:S(2)}) collective-permute-start(bf16[128,2176]{0,1:T(8,128)(2,1)} %collective-permute-done.15), channel_id=1, source_target_pairs={{0,1},{1,2},{2,3},{3,4},{4,5},{5,6},{6,7},{7,8},{8,9},{9,10},{10,1... | collective-permute-start | bytes 1671176 | tf_op jit(solution)/shard_map/ppermute | solution.py:32
  133.8 11.3 %collective-permute-start.7 = (bf16[128,2176]{0,1:T(8,128)(2,1)}, bf16[128,2176]{0,1:T(8,128)(2,1)}, u32[]{:S(2)}, u32[]{:S(2)}) collective-permute-start(bf16[128,2176]{0,1:T(8,128)(2,1)} %collective-permute-done.6), channel_id=1, source_target_pairs={{0,31},{1,0},{2,1},{3,2},{4,3},{5,4},{6,5},{7,6},{8,7},{9,8},{10,9... | collective-permute-start | bytes 1671176 | tf_op jit(solution)/shard_map/ppermute | solution.py:32
  139.8 13.0 %collective-permute-start.17 = (bf16[128,2176]{0,1:T(8,128)(2,1)}, bf16[128,2176]{0,1:T(8,128)(2,1)S(1)}, u32[]{:S(2)}, u32[]{:S(2)}) collective-permute-start(bf16[128,2176]{0,1:T(8,128)(2,1)} %collective-permute-done.16), channel_id=1, source_target_pairs={{0,1},{1,2},{2,3},{3,4},{4,5},{5,6},{6,7},{7,8},{8,9},{9,10},{10,1... | collective-permute-start | bytes 1671176 | tf_op jit(solution)/shard_map/ppermute | solution.py:32
  145.2 15.6 %collective-permute-start.8 = (bf16[128,2176]{0,1:T(8,128)(2,1)}, bf16[128,2176]{0,1:T(8,128)(2,1)}, u32[]{:S(2)}, u32[]{:S(2)}) collective-permute-start(bf16[128,2176]{0,1:T(8,128)(2,1)} %collective-permute-done.7), channel_id=1, source_target_pairs={{0,31},{1,0},{2,1},{3,2},{4,3},{5,4},{6,5},{7,6},{8,7},{9,8},{10,9... | collective-permute-start | bytes 1671176 | tf_op jit(solution)/shard_map/ppermute | solution.py:32
  164.6 3.2 copy-start.38
  164.6 3.4 copy-start.43
  164.6 3.5 copy-start.44
  164.6 3.7 copy-start.2
  167.8 3.4 copy-start.30
  168.2 3.2 copy-start.28
  168.5 3.2 copy-start.26
  169.8 2.1 copy-start.22
  171.7 1.2 copy-start.3
  172.0 10.4 %copy-start.10 = (bf16[128,2176]{0,1:T(8,128)(2,1)S(1)}, bf16[128,2176]{0,1:T(8,128)(2,1)}, u32[]{:S(2)}) copy-start(bf16[128,2176]{0,1:T(8,128)(2,1)} %copy-done.9) | copy-start | bytes 1671172
  172.3 10.4 %copy-start.14 = (bf16[128,2176]{0,1:T(8,128)(2,1)S(1)}, bf16[128,2176]{0,1:T(8,128)(2,1)}, u32[]{:S(2)}) copy-start(bf16[128,2176]{0,1:T(8,128)(2,1)} %copy-done.13) | copy-start | bytes 1671172
  172.6 10.3 %copy-start.18 = (bf16[128,2176]{0,1:T(8,128)(2,1)S(1)}, bf16[128,2176]{0,1:T(8,128)(2,1)}, u32[]{:S(2)}) copy-start(bf16[128,2176]{0,1:T(8,128)(2,1)} %copy-done.17) | copy-start | bytes 1671172
  172.9 10.3 %copy-start.20 = (bf16[128,2176]{0,1:T(8,128)(2,1)S(1)}, bf16[128,2176]{0,1:T(8,128)(2,1)}, u32[]{:S(2)}) copy-start(bf16[128,2176]{0,1:T(8,128)(2,1)} %copy-done.19) | copy-start | bytes 1671172
  173.1 10.3 %copy-start.24 = (bf16[128,2176]{0,1:T(8,128)(2,1)S(1)}, bf16[128,2176]{0,1:T(8,128)(2,1)}, u32[]{:S(2)}) copy-start(bf16[128,2176]{0,1:T(8,128)(2,1)} %copy-done.23) | copy-start | bytes 1671172
  173.1 20.2 %collective-permute-start.21 = (bf16[64,2048]{1,0:T(8,128)(2,1)S(1)}, bf16[64,2048]{1,0:T(8,128)(2,1)S(1)}, u32[]{:S(2)}, u32[]{:S(2)}) collective-permute-start(bf16[64,2048]{1,0:T(8,128)(2,1)S(1)} %copy-done.34), channel_id=1, source_target_pairs={{0,4},{1,5},{2,6},{3,7},{4,8},{5,9},{6,10},{7,11},{8,12},{9,13},{1... | collective-permute-start | bytes 786440 | tf_op jit(solution)/shard_map/ppermute | solution.py:32
  175.1 13.8 %collective-permute-start.18 = (bf16[48,2048]{1,0:T(8,128)(2,1)S(1)}, bf16[48,2048]{1,0:T(8,128)(2,1)S(1)}, u32[]{:S(2)}, u32[]{:S(2)}) collective-permute-start(bf16[48,2048]{1,0:T(8,128)(2,1)S(1)} %split.119), channel_id=1, source_target_pairs={{0,28},{1,29},{2,30},{3,31},{4,0},{5,1},{6,2},{7,3},{8,4},{9,5},{1... | collective-permute-start | bytes 589832 | tf_op jit(solution)/shard_map/ppermute | solution.py:32
  186.3 7.1 %copy-start.36 = (bf16[16,2048]{1,0:T(8,128)(2,1)S(1)}, bf16[16,2048]{1,0:T(8,128)(2,1)}, u32[]{:S(2)}) copy-start(bf16[16,2048]{1,0:T(8,128)(2,1)} %get-tuple-element.17) | copy-start | bytes 196612
  186.3 7.1 %copy-start.37 = (bf16[16,2048]{1,0:T(8,128)(2,1)S(1)}, bf16[16,2048]{1,0:T(8,128)(2,1)}, u32[]{:S(2)}) copy-start(bf16[16,2048]{1,0:T(8,128)(2,1)} %get-tuple-element.18) | copy-start | bytes 196612
  186.3 9.1 %copy-start.4 = (bf16[19,16,768]{2,1,0:T(8,128)(2,1)S(1)}, bf16[19,16,768]{2,1,0:T(8,128)(2,1)}, u32[]{:S(2)}) copy-start(bf16[19,16,768]{2,1,0:T(8,128)(2,1)} %slice.327) | copy-start | bytes 1400836
  188.9 8.4 %copy-start.6 = (bf16[304,2048]{1,0:T(8,128)(2,1)}, bf16[304,2048]{1,0:T(8,128)(2,1)S(1)}, u32[]{:S(2)}) copy-start(bf16[304,2048]{1,0:T(8,128)(2,1)S(1)} %fusion.5) | copy-start | bytes 3735556
  189.0 14.4 %collective-permute-start.19 = (bf16[48,2048]{1,0:T(8,128)(2,1)S(1)}, bf16[48,2048]{1,0:T(8,128)(2,1)S(1)}, u32[]{:S(2)}, u32[]{:S(2)}) collective-permute-start(bf16[48,2048]{1,0:T(8,128)(2,1)S(1)} %pad_maximum_fusion.4), channel_id=1, source_target_pairs={{0,30},{1,31},{2,0},{3,1},{4,2},{5,3},{6,4},{7,5},{8,6},{9,7},{10,... | collective-permute-start | bytes 589832 | tf_op jit(solution)/shard_map/ppermute | solution.py:32
  193.4 13.3 %collective-permute-start.22 = (bf16[64,2048]{1,0:T(8,128)(2,1)S(1)}, bf16[64,2048]{1,0:T(8,128)(2,1)S(1)}, u32[]{:S(2)}, u32[]{:S(2)}) collective-permute-start(bf16[64,2048]{1,0:T(8,128)(2,1)S(1)} %pad_maximum_fusion.2), channel_id=1, source_target_pairs={{0,2},{1,3},{2,4},{3,5},{4,6},{5,7},{6,8},{7,9},{8,10},{9,11},{10,... | collective-permute-start | bytes 786440 | tf_op jit(solution)/shard_map/ppermute | solution.py:32
  195.3 11.4 %copy-start.35 = (bf16[16,2048]{1,0:T(8,128)(2,1)S(1)}, bf16[16,2048]{1,0:T(8,128)(2,1)}, u32[]{:S(2)}) copy-start(bf16[16,2048]{1,0:T(8,128)(2,1)} %get-tuple-element.16) | copy-start | bytes 196612
  203.4 6.7 %collective-permute-start.20 = (bf16[48,2048]{1,0:T(8,128)(2,1)S(1)}, bf16[48,2048]{1,0:T(8,128)(2,1)S(1)}, u32[]{:S(2)}, u32[]{:S(2)}) collective-permute-start(bf16[48,2048]{1,0:T(8,128)(2,1)S(1)} %pad_maximum_fusion.5), channel_id=1, source_target_pairs={{0,31},{1,0},{2,1},{3,2},{4,3},{5,4},{6,5},{7,6},{8,7},{9,8},{10,9... | collective-permute-start | bytes 589832 | tf_op jit(solution)/shard_map/ppermute | solution.py:32
  206.8 15.3 %collective-permute-start.23 = (bf16[64,2048]{1,0:T(8,128)(2,1)S(1)}, bf16[64,2048]{1,0:T(8,128)(2,1)S(1)}, u32[]{:S(2)}, u32[]{:S(2)}) collective-permute-start(bf16[64,2048]{1,0:T(8,128)(2,1)S(1)} %pad_maximum_fusion.3), channel_id=1, source_target_pairs={{0,1},{1,2},{2,3},{3,4},{4,5},{5,6},{6,7},{7,8},{8,9},{9,10},{10,1... | collective-permute-start | bytes 786440 | tf_op jit(solution)/shard_map/ppermute | solution.py:32
  222.2 1.9 copy-start.8
  224.9 2.3 copy-start.5
  224.9 2.3 copy-start.7
  230.7 32.2 %copy-start.40 = (f32[32,128]{1,0:T(8,128)S(1)}, f32[32,128]{1,0:T(8,128)}, u32[]{:S(2)}) copy-start(f32[32,128]{1,0:T(8,128)} %copy-done.39) | copy-start | bytes 49156
  231.4 31.4 %all-to-all-start = ((f32[32,1,16]{2,1,0:T(1,128)}), f32[32,1,16]{2,1,0:T(1,128)S(1)}, u32[]{:S(2)}, u32[]{:S(2)}) async-start(f32[32,1,16]{2,1,0:T(1,128)} %bitcast.6), calls=%async_computation | async-start | bytes 32768 | tf_op jit(solution)/shard_map/all_to_all | solution.py:143
  265.8 23.1 %copy-start.31 = (bf16[208,768]{1,0:T(8,128)(2,1)S(1)}, bf16[208,768]{1,0:T(8,128)(2,1)}, u32[]{:S(2)}) copy-start(bf16[208,768]{1,0:T(8,128)(2,1)} %get-tuple-element.14) | copy-start | bytes 958468
  267.9 32.5 %all-to-all-start.1 = ((bf16[32,64,128]{2,1,0:T(8,128)(2,1)}), bf16[32,64,128]{2,1,0:T(8,128)(2,1)}, u32[]{:S(2)}, u32[]{:S(2)}) async-start(bf16[32,64,128]{2,1,0:T(8,128)(2,1)} %bitcast.55), calls=%async_computation.1 | async-start | bytes 1048576 | tf_op jit(solution)/shard_map/all_to_all | solution.py:21
  290.0 16.1 %copy-start.33 = (bf16[128,128]{1,0:T(8,128)(2,1)S(1)}, bf16[128,128]{1,0:T(8,128)(2,1)}, u32[]{:S(2)}) copy-start(bf16[128,128]{1,0:T(8,128)(2,1)} %copy-done.32) | copy-start | bytes 98308
  302.3 24.7 %all-to-all-start.2 = ((bf16[32,2,128]{2,1,0:T(2,128)(2,1)}), bf16[32,2,128]{2,1,0:T(2,128)(2,1)S(1)}, u32[]{:S(2)}, u32[]{:S(2)}) async-start(bf16[32,2,128]{2,1,0:T(2,128)(2,1)} %reshape.39), calls=%async_computation.2 | async-start | bytes 32768 | tf_op jit(solution)/shard_map/all_to_all | solution.py:21
  (9 other events, 7.7 us)
Sparse Core Ops, SparseCore 0:
  230.8 133.5 reduce-scatter.1

commit v3 on v2

--- a/solution.py
+++ b/solution.py
@@ -51,16 +51,22 @@
     ).astype(BF16)
 
 
-def spread(rows, capacity, way):
-    parts = {k + 1: [(0, r)] for k, r in enumerate(jnp.split(rows, rows.shape[0] // capacity))}
+def spread(pick_far, targets, way):
     step = 4
-    while step:
+    sent = [(k + 1, 0, None) for k in range(step - 1, len(targets))]
+    rows = pick_far(targets[step - 1 :])
+    got = shift(rows, way * step)
+    rest = jnp.split(pick_far(targets[: step - 1]), step - 1)
+    parts = {k + 1: [(0, r)] for k, r in enumerate(rest)}
+    while True:
+        for (k, far, _), r in zip(sent, jnp.split(got, len(sent))):
+            parts.setdefault(k - step, []).append((far + step, r))
+        step //= 2
+        if not step:
+            break
         sent = [(k, far, r) for k in sorted(parts) if k >= step for far, r in parts[k]]
         parts = {k: v for k, v in parts.items() if k < step}
         got = shift(jnp.concatenate([r for _, _, r in sent], axis=0), way * step)
-        for (k, far, _), r in zip(sent, jnp.split(got, len(sent))):
-            parts.setdefault(k - step, []).append((far + step, r))
-        step //= 2
     return [r for _, r in sorted(parts[0], key=lambda pair: pair[0])]
 
 
@@ -71,6 +77,43 @@
 
 def across(hidden, rows):
     return lax.dot_general(hidden, rows, (((0,), (0,)), ((), ())), preferred_element_type=F32)
+
+
+SIDE = 4
+
+
+def from_peers(parts, mine, place, perm_of, count):
+    total = lax.dynamic_index_in_dim(parts, mine, 0, keepdims=False).astype(F32)
+    for step in range(1, count):
+        out = lax.dynamic_index_in_dim(parts, (mine + step) % count, 0, keepdims=False)
+        got = lax.ppermute(out, "dp", [(i, perm_of(i, step)) for i in range(place)])
+        total = total + got.astype(F32)
+    return total
+
+
+def sum_over_cores(partial):
+    size = lax.axis_size("dp")
+    width = partial.shape[1]
+    core = lax.axis_index("dp") % 2
+    parts = jnp.moveaxis(partial.reshape(size // 2, 2, -1, width), 1, 0)
+    return from_peers(parts, core, size, lambda i, step: i ^ 1, 2).astype(BF16)
+
+
+def sum_over_chips(halves):
+    size = lax.axis_size("dp")
+    at = lax.axis_index("dp") // 2
+    rows, width = halves.shape[1:]
+    sides = size // 2 // SIDE
+
+    def in_x(i, step):
+        return (i // (2 * SIDE)) * 2 * SIDE + ((i // 2 % SIDE + step) % SIDE) * 2 + i % 2
+
+    def in_y(i, step):
+        return ((i // (2 * SIDE) + step) % sides) * 2 * SIDE + i % (2 * SIDE)
+
+    by_x = jnp.moveaxis(halves.reshape(sides, SIDE, rows, width), 1, 0)
+    row = from_peers(by_x, at % SIDE, size, in_x, SIDE).astype(BF16)
+    return from_peers(row, at // SIDE, size, in_y, sides)
 
 
 def shards(tokens_in, out_grad, expert_ids, rest_scores, router_weight, down_weight, saved_hidden):
@@ -114,10 +157,12 @@
 
     far_up = list(range(NEAR + 1, n // 2 + 1))
     far_down = [n - k for k in far_up[:-1]]
-    up_rows = pick(tables(up[NEAR][:, width:], n, far_up, capacity), up[NEAR], width)
-    low_rows = pick(tables(down[NEAR][:, width:], n, far_down, capacity), down[NEAR], width)
-    top = spread(up_rows, capacity, 1)
-    low = spread(low_rows, capacity, -1)
+
+    def far_of(block):
+        return lambda lanes: pick(tables(block[:, width:], n, lanes, capacity), block, width)
+
+    top = spread(far_of(up[NEAR]), far_up, 1)
+    low = spread(far_of(down[NEAR]), far_down, -1)
 
     blocks = [(h, up[h]) for h in range(NEAR, 0, -1)] + [(0, own)]
     blocks += [(n - h, down[h]) for h in range(1, NEAR + 1)]
@@ -142,7 +187,8 @@
     scores, far = lax.optimization_barrier((turned(scores, home), far))
     returned = lax.all_to_all(scores, "expert", split_axis=0, concat_axis=0, tiled=True)[:, 0]
     partial = (across(hidden[:cut], near) + across(hidden[cut:], far)).astype(BF16)
-    down_grad = lax.psum_scatter(partial, "dp", scatter_dimension=0, tiled=True).astype(F32)
+    halves = sum_over_cores(partial)
+    down_grad = sum_over_chips(halves)
     hid_grad = jnp.concatenate([hid_near, hid_far], axis=0)
     hidden_grad = turned(hid_grad.reshape(n, capacity, hidden_units), home)
 

time: 376 us -> 365 us (0.971)
  waiting for transfers between devices: 163 us -> 108 us
  starting transfers between devices: 130 us -> 163 us
  matrix products: 34.7 us -> 47.9 us
  between operations: 15 us -> 1.83 us
  local copies, waits for them, and re-layouts: 15.3 us -> 24 us
    reduce_scatter x1 -> x0, waiting for transfers between devices: 36.7 us -> none  [shards(): lax.psum_scatter(partial, 'dp', scatter_dimension=0, tiled=True).astype(F32)]
    ppermute x0 -> x7, starting transfers between devices: none -> 33.8 us  [from_peers(): got = lax.ppermute(out, 'dp', [(i, perm_of(i, step)) for i in range(place)])]
    dot_general x21 -> x23, matrix products: 15.7 us -> 28.8 us  [pick(): lax.dot_general(table, block[:, :width], (((1,), (0,)), ((), ())), prefer...]
    all_to_all x2, starting transfers between devices: 24.8 us -> 12.4 us  [sum_at_owner(): lax.all_to_all(parts, axis, split_axis=0, concat_axis=0, tiled=True)]
    ppermute x24, waiting for transfers between devices: 76.8 us -> 65.8 us  [shift(): lax.ppermute(value, 'expert', [(k, (k + step) % n) for k in range(n)])]
    all_to_all x2, waiting for transfers between devices: 27.9 us -> 18.6 us  [sum_at_owner(): lax.all_to_all(parts, axis, split_axis=0, concat_axis=0, tiled=True)]
    ppermute x24, starting transfers between devices: 94.8 us -> 103 us  [shift(): lax.ppermute(value, 'expert', [(k, (k + step) % n) for k in range(n)])]
    unnamed x105 -> x117, local copies, waits for them, and re-layouts: 6.96 us -> 13.2 us
  transfers between devices with their start and end apart: 28 -> 34, of which waited for: 18 -> 20; matrix products, arithmetic and copies ran while one was open for 9% -> 13% of each run, Pallas kernels for 0% -> 0%
where the time goes in v3:
time: 365 us; the launch traced here: 361 us
  starting transfers between devices  163 us (45%)
  waiting for transfers between devices  108 us (30%)
  matrix products  47.9 us (13%)
  local copies, waits for them, and re-layouts  24 us (7%)
  other arithmetic  15.9 us (4%)
    ppermute x24, starting transfers between devices, shift(): lax.ppermute(value, 'expert', [(k, (k + step) % n) for k in range(n)])  103 us
    ppermute x24, waiting for transfers between devices, shift(): lax.ppermute(value, 'expert', [(k, (k + step) % n) for k in range(n)])  65.8 us
    ppermute x7, starting transfers between devices, from_peers(): got = lax.ppermute(out, 'dp', [(i, perm_of(i, step)) for i in range(place)])  33.8 us
    dot_general x23, matrix products, pick(): lax.dot_general(table, block[:, :width], (((1,), (0,)), ((), ())), prefer...  28.8 us
    all_to_all x1, waiting for transfers between devices, shards(): lax.all_to_all(scores, 'expert', split_axis=0, concat_axis=0, tiled=True)  21 us
    all_to_all x2, waiting for transfers between devices, sum_at_owner(): lax.all_to_all(parts, axis, split_axis=0, concat_axis=0, tiled=True)  18.6 us
    all_to_all x1, starting transfers between devices, shards(): lax.all_to_all(scores, 'expert', split_axis=0, concat_axis=0, tiled=True)  13.6 us
    unnamed x117, local copies, waits for them, and re-layouts  13.2 us
  transfers between devices with their start and end apart: 34, of which 20 were waited for; matrix products, arithmetic and copies ran while one was open for 13% of the time, Pallas kernels for 0%

profile of v3, /device:TPU:1, one launch (start us, length us, event | category | flops | bytes accessed | tf_op | source)
XLA Modules:
  0.0 360.7 jit_solution(7857341458327562762)
XLA Ops:
  3.4 2.0 copy.32
  6.6 4.4 %collective-permute-start.9 = (bf16[128,2176]{0,1:T(8,128)(2,1)S(1)}, bf16[128,2176]{0,1:T(8,128)(2,1)S(1)}, u32[]{:S(2)}, u32[]{:S(2)}) collective-permute-start(bf16[128,2176]{0,1:T(8,128)(2,1)S(1)} %pad_maximum_fusion.1), channel_id=1, source_target_pairs={{0,1},{1,2},{2,3},{3,4},{4,5},{5,6},{6,7},{7,8},{8,9},{9,10},{10,1... | collective-permute-start | bytes 1671176 | tf_op jit(solution)/shard_map/ppermute | solution.py:32
  10.9 16.8 %collective-permute-start = (bf16[128,2176]{0,1:T(8,128)(2,1)S(1)}, bf16[128,2176]{0,1:T(8,128)(2,1)S(1)}, u32[]{:S(2)}, u32[]{:S(2)}) collective-permute-start(bf16[128,2176]{0,1:T(8,128)(2,1)S(1)} %pad_maximum_fusion.1), channel_id=1, source_target_pairs={{0,31},{1,0},{2,1},{3,2},{4,3},{5,4},{6,5},{7,6},{8,7},{9,8},{10,9... | collective-permute-start | bytes 1671176 | tf_op jit(solution)/shard_map/ppermute | solution.py:32
  27.7 10.4 %collective-permute-done.9 = bf16[128,2176]{0,1:T(8,128)(2,1)S(1)} collective-permute-done((bf16[128,2176]{0,1:T(8,128)(2,1)S(1)}, bf16[128,2176]{0,1:T(8,128)(2,1)S(1)}, u32[]{:S(2)}, u32[]{:S(2)}) %collective-permute-start.9) | collective-permute-done | bytes 557088 | tf_op jit(solution)/shard_map/ppermute | solution.py:32
  38.1 1.9 collective-permute-start.10
  40.8 4.6 %collective-permute-start.1 = (bf16[128,2176]{0,1:T(8,128)(2,1)S(1)}, bf16[128,2176]{0,1:T(8,128)(2,1)S(1)}, u32[]{:S(2)}, u32[]{:S(2)}) collective-permute-start(bf16[128,2176]{0,1:T(8,128)(2,1)S(1)} %collective-permute-done), channel_id=1, source_target_pairs={{0,31},{1,0},{2,1},{3,2},{4,3},{5,4},{6,5},{7,6},{8,7},{9,8},{10,9... | collective-permute-start | bytes 1671176 | tf_op jit(solution)/shard_map/ppermute | solution.py:32
  45.4 8.7 %collective-permute-done.10 = bf16[128,2176]{0,1:T(8,128)(2,1)S(1)} collective-permute-done((bf16[128,2176]{0,1:T(8,128)(2,1)S(1)}, bf16[128,2176]{0,1:T(8,128)(2,1)S(1)}, u32[]{:S(2)}, u32[]{:S(2)}) %collective-permute-start.10) | collective-permute-done | bytes 557088 | tf_op jit(solution)/shard_map/ppermute | solution.py:32
  54.1 1.9 collective-permute-start.11
  56.9 5.1 %collective-permute-start.2 = (bf16[128,2176]{0,1:T(8,128)(2,1)S(1)}, bf16[128,2176]{0,1:T(8,128)(2,1)S(1)}, u32[]{:S(2)}, u32[]{:S(2)}) collective-permute-start(bf16[128,2176]{0,1:T(8,128)(2,1)S(1)} %collective-permute-done.1), channel_id=1, source_target_pairs={{0,31},{1,0},{2,1},{3,2},{4,3},{5,4},{6,5},{7,6},{8,7},{9,8},{10,9... | collective-permute-start | bytes 1671176 | tf_op jit(solution)/shard_map/ppermute | solution.py:32
  62.0 7.3 %collective-permute-done.11 = bf16[128,2176]{0,1:T(8,128)(2,1)S(1)} collective-permute-done((bf16[128,2176]{0,1:T(8,128)(2,1)S(1)}, bf16[128,2176]{0,1:T(8,128)(2,1)S(1)}, u32[]{:S(2)}, u32[]{:S(2)}) %collective-permute-start.11) | collective-permute-done | bytes 557088 | tf_op jit(solution)/shard_map/ppermute | solution.py:32
  69.3 1.9 collective-permute-start.12
  72.4 5.3 %collective-permute-start.3 = (bf16[128,2176]{0,1:T(8,128)(2,1)S(1)}, bf16[128,2176]{0,1:T(8,128)(2,1)S(1)}, u32[]{:S(2)}, u32[]{:S(2)}) collective-permute-start(bf16[128,2176]{0,1:T(8,128)(2,1)S(1)} %collective-permute-done.2), channel_id=1, source_target_pairs={{0,31},{1,0},{2,1},{3,2},{4,3},{5,4},{6,5},{7,6},{8,7},{9,8},{10,9... | collective-permute-start | bytes 1671176 | tf_op jit(solution)/shard_map/ppermute | solution.py:32
  77.7 5.9 %collective-permute-done.12 = bf16[128,2176]{0,1:T(8,128)(2,1)S(1)} collective-permute-done((bf16[128,2176]{0,1:T(8,128)(2,1)S(1)}, bf16[128,2176]{0,1:T(8,128)(2,1)S(1)}, u32[]{:S(2)}, u32[]{:S(2)}) %collective-permute-start.12) | collective-permute-done | bytes 557088 | tf_op jit(solution)/shard_map/ppermute | solution.py:32
  83.6 1.9 collective-permute-start.13
  87.2 5.3 %collective-permute-start.4 = (bf16[128,2176]{0,1:T(8,128)(2,1)S(1)}, bf16[128,2176]{0,1:T(8,128)(2,1)S(1)}, u32[]{:S(2)}, u32[]{:S(2)}) collective-permute-start(bf16[128,2176]{0,1:T(8,128)(2,1)S(1)} %collective-permute-done.3), channel_id=1, source_target_pairs={{0,31},{1,0},{2,1},{3,2},{4,3},{5,4},{6,5},{7,6},{8,7},{9,8},{10,9... | collective-permute-start | bytes 1671176 | tf_op jit(solution)/shard_map/ppermute | solution.py:32
  92.5 4.5 %collective-permute-done.13 = bf16[128,2176]{0,1:T(8,128)(2,1)S(1)} collective-permute-done((bf16[128,2176]{0,1:T(8,128)(2,1)S(1)}, bf16[128,2176]{0,1:T(8,128)(2,1)S(1)}, u32[]{:S(2)}, u32[]{:S(2)}) %collective-permute-start.13) | collective-permute-done | bytes 557088 | tf_op jit(solution)/shard_map/ppermute | solution.py:32
  97.1 1.9 collective-permute-start.14
  101.2 5.3 %collective-permute-start.5 = (bf16[128,2176]{0,1:T(8,128)(2,1)S(1)}, bf16[128,2176]{0,1:T(8,128)(2,1)S(1)}, u32[]{:S(2)}, u32[]{:S(2)}) collective-permute-start(bf16[128,2176]{0,1:T(8,128)(2,1)S(1)} %collective-permute-done.4), channel_id=1, source_target_pairs={{0,31},{1,0},{2,1},{3,2},{4,3},{5,4},{6,5},{7,6},{8,7},{9,8},{10,9... | collective-permute-start | bytes 1671176 | tf_op jit(solution)/shard_map/ppermute | solution.py:32
  106.5 3.2 collective-permute-done.14
  109.7 1.9 collective-permute-start.15
  111.6 1.9 collective-permute-done.5
  113.5 5.3 %collective-permute-start.6 = (bf16[128,2176]{0,1:T(8,128)(2,1)S(1)}, bf16[128,2176]{0,1:T(8,128)(2,1)}, u32[]{:S(2)}, u32[]{:S(2)}) collective-permute-start(bf16[128,2176]{0,1:T(8,128)(2,1)S(1)} %collective-permute-done.5), channel_id=1, source_target_pairs={{0,31},{1,0},{2,1},{3,2},{4,3},{5,4},{6,5},{7,6},{8,7},{9,8},{10,9... | collective-permute-start | bytes 1671176 | tf_op jit(solution)/shard_map/ppermute | solution.py:32
  118.9 2.4 collective-permute-done.15
  121.3 1.9 collective-permute-start.16
  123.2 2.1 collective-permute-done.6
  125.3 5.1 %collective-permute-start.7 = (bf16[128,2176]{0,1:T(8,128)(2,1)}, bf16[128,2176]{0,1:T(8,128)(2,1)}, u32[]{:S(2)}, u32[]{:S(2)}) collective-permute-start(bf16[128,2176]{0,1:T(8,128)(2,1)} %collective-permute-done.6), channel_id=1, source_target_pairs={{0,31},{1,0},{2,1},{3,2},{4,3},{5,4},{6,5},{7,6},{8,7},{9,8},{10,9... | collective-permute-start | bytes 1671176 | tf_op jit(solution)/shard_map/ppermute | solution.py:32
  135.3 2.3 collective-permute-done.7
  137.6 5.0 %collective-permute-start.8 = (bf16[128,2176]{0,1:T(8,128)(2,1)}, bf16[128,2176]{0,1:T(8,128)(2,1)S(1)}, u32[]{:S(2)}, u32[]{:S(2)}) collective-permute-start(bf16[128,2176]{0,1:T(8,128)(2,1)} %collective-permute-done.7), channel_id=1, source_target_pairs={{0,31},{1,0},{2,1},{3,2},{4,3},{5,4},{6,5},{7,6},{8,7},{9,8},{10,9... | collective-permute-start | bytes 1671176 | tf_op jit(solution)/shard_map/ppermute | solution.py:32
  146.2 4.8 %collective-permute-done.8 = bf16[128,2176]{0,1:T(8,128)(2,1)S(1)} collective-permute-done((bf16[128,2176]{0,1:T(8,128)(2,1)}, bf16[128,2176]{0,1:T(8,128)(2,1)S(1)}, u32[]{:S(2)}, u32[]{:S(2)}) %collective-permute-start.8) | collective-permute-done | bytes 557088 | tf_op jit(solution)/shard_map/ppermute | solution.py:32
  161.2 2.1 convolution_convert_fusion.3
  165.8 2.2 convolution_convert_fusion.2
  168.1 1.9 collective-permute-start.21
  170.9 2.1 convolution_convert_fusion.4
  173.0 7.3 %collective-permute-start.18 = (bf16[48,2048]{1,0:T(8,128)(2,1)}, bf16[48,2048]{1,0:T(8,128)(2,1)}, u32[]{:S(2)}, u32[]{:S(2)}) collective-permute-start(bf16[48,2048]{1,0:T(8,128)(2,1)} %convolution_convert_fusion.4), channel_id=1, source_target_pairs={{0,28},{1,29},{2,30},{3,31},{4,0},{5,1},{6,2},{7,3},{8,4},{9,5},{1... | collective-permute-start | bytes 589832 | tf_op jit(solution)/shard_map/ppermute | solution.py:32
  181.2 2.2 convolution_convert_fusion.5
  184.4 2.0 fusion.14
  186.4 2.0 fusion.13
  194.6 1.9 fusion.8
  196.5 2.0 fusion.7
  201.1 3.2 collective-permute-start.19
  205.3 2.9 collective-permute-start.22
  208.3 2.0 fusion.167
  210.3 6.1 %collective-permute-start.20 = (bf16[48,2048]{1,0:T(8,128)(2,1)S(1)}, bf16[48,2048]{1,0:T(8,128)(2,1)S(1)}, u32[]{:S(2)}, u32[]{:S(2)}) collective-permute-start(bf16[48,2048]{1,0:T(8,128)(2,1)S(1)} %pad_maximum_fusion.5), channel_id=1, source_target_pairs={{0,31},{1,0},{2,1},{3,2},{4,3},{5,4},{6,5},{7,6},{8,7},{9,8},{10,9... | collective-permute-start | bytes 589832 | tf_op jit(solution)/shard_map/ppermute | solution.py:32
  216.5 4.2 %collective-permute-start.23 = (bf16[64,2048]{1,0:T(8,128)(2,1)S(1)}, bf16[64,2048]{1,0:T(8,128)(2,1)S(1)}, u32[]{:S(2)}, u32[]{:S(2)}) collective-permute-start(bf16[64,2048]{1,0:T(8,128)(2,1)S(1)} %pad_maximum_fusion.3), channel_id=1, source_target_pairs={{0,1},{1,2},{2,3},{3,4},{4,5},{5,6},{6,7},{7,8},{8,9},{9,10},{10,1... | collective-permute-start | bytes 786440 | tf_op jit(solution)/shard_map/ppermute | solution.py:32
  222.2 7.1 %collective-permute-done.23 = bf16[64,2048]{1,0:T(8,128)(2,1)S(1)} collective-permute-done((bf16[64,2048]{1,0:T(8,128)(2,1)S(1)}, bf16[64,2048]{1,0:T(8,128)(2,1)S(1)}, u32[]{:S(2)}, u32[]{:S(2)}) %collective-permute-start.23) | collective-permute-done | bytes 262176 | tf_op jit(solution)/shard_map/ppermute | solution.py:32
  230.3 1.9 fusion.168
  233.0 2.3 fusion.175
  239.3 12.7 %collective-permute-start.24 = (bf16[16,24,2048]{2,1,0:T(8,128)(2,1)}, bf16[16,24,2048]{2,1,0:T(8,128)(2,1)}, u32[]{:S(2)}, u32[]{:S(2)}) collective-permute-start(bf16[16,24,2048]{2,1,0:T(8,128)(2,1)} %dynamic-slice_bitcast_fusion), channel_id=1, source_target_pairs={{0,32},{32,0},{64,96},{96,64},{128,160},{160,128},{192,224},{224,1... | collective-permute-start | bytes 4718600 | tf_op jit(solution)/shard_map/ppermute | solution.py:89
  252.0 13.6 %all-to-all-start = ((f32[32,1,16]{2,1,0:T(1,128)}), f32[32,1,16]{2,1,0:T(1,128)S(1)}, u32[]{:S(2)}, u32[]{:S(2)}) async-start(f32[32,1,16]{2,1,0:T(1,128)} %bitcast.6), calls=%async_computation | async-start | bytes 32768 | tf_op jit(solution)/shard_map/all_to_all | solution.py:188
  265.8 21.0 %all-to-all-done = f32[32,1,16]{2,1,0:T(1,128)S(1)} async-done(((f32[32,1,16]{2,1,0:T(1,128)}), f32[32,1,16]{2,1,0:T(1,128)S(1)}, u32[]{:S(2)}, u32[]{:S(2)}) %all-to-all-start) | async-done | bytes 2080 | tf_op jit(solution)/shard_map/all_to_all | solution.py:188
  287.6 2.1 fusion.5
  289.7 2.1 copy.34
  291.8 8.6 %all-to-all-start.1 = ((bf16[32,64,128]{2,1,0:T(8,128)(2,1)}), bf16[32,64,128]{2,1,0:T(8,128)(2,1)}, u32[]{:S(2)}, u32[]{:S(2)}) async-start(bf16[32,64,128]{2,1,0:T(8,128)(2,1)} %bitcast.89), calls=%async_computation.1 | async-start | bytes 1048576 | tf_op jit(solution)/shard_map/all_to_all | solution.py:21
  300.5 2.5 fusion
  304.0 3.2 collective-permute-start.25
  307.3 4.3 %collective-permute-start.26 = (bf16[4,24,2048]{2,1,0:T(8,128)(2,1)}, bf16[4,24,2048]{2,1,0:T(8,128)(2,1)}, u32[]{:S(2)}, u32[]{:S(2)}) collective-permute-start(bf16[4,24,2048]{2,1,0:T(8,128)(2,1)} %get-tuple-element.14), channel_id=1, source_target_pairs={{0,128},{32,160},{64,192},{96,224},{128,0},{160,32},{192,64},{224,... | collective-permute-start | bytes 1179656 | tf_op jit(solution)/shard_map/ppermute | solution.py:89
  311.6 3.1 collective-permute-start.27
  319.3 3.7 %all-to-all-start.2 = ((bf16[32,2,128]{2,1,0:T(2,128)(2,1)}), bf16[32,2,128]{2,1,0:T(2,128)(2,1)S(1)}, u32[]{:S(2)}, u32[]{:S(2)}) async-start(bf16[32,2,128]{2,1,0:T(2,128)(2,1)} %reshape.67), calls=%async_computation.2 | async-start | bytes 32768 | tf_op jit(solution)/shard_map/all_to_all | solution.py:21
  323.0 2.2 convolution_convert_fusion.1
  325.2 18.6 %all-to-all-done.2 = bf16[32,2,128]{2,1,0:T(2,128)(2,1)S(1)} async-done(((bf16[32,2,128]{2,1,0:T(2,128)(2,1)}), bf16[32,2,128]{2,1,0:T(2,128)(2,1)S(1)}, u32[]{:S(2)}, u32[]{:S(2)}) %all-to-all-start.2) | async-done | bytes 16416 | tf_op jit(solution)/shard_map/all_to_all | solution.py:21
  346.2 3.1 collective-permute-start.28
  349.3 4.4 %collective-permute-start.29 = (bf16[24,2048]{1,0:T(8,128)(2,1)S(1)}, bf16[24,2048]{1,0:T(8,128)(2,1)S(1)}, u32[]{:S(2)}, u32[]{:S(2)}) collective-permute-start(bf16[24,2048]{1,0:T(8,128)(2,1)S(1)} %get-tuple-element.21), channel_id=1, source_target_pairs={{0,512},{32,544},{64,576},{96,608},{128,640},{160,672},{192,704},{... | collective-permute-start | bytes 294920 | tf_op jit(solution)/shard_map/ppermute | solution.py:89
  353.6 3.0 collective-permute-start.30
  357.3 2.6 collective-permute-done.30
  (211 shorter events, 61.2 us)
Async XLA Ops:
  0.6 207.6 %copy-start = (bf16[1,768,2048]{2,1,0:T(8,128)(2,1)S(1)}, bf16[1,768,2048]{2,1,0:T(8,128)(2,1)}, u32[]{:S(2)}) copy-start(bf16[1,768,2048]{2,1,0:T(8,128)(2,1)} %param.22) | copy-start | bytes 9437188
  6.6 31.5 %collective-permute-start.9 = (bf16[128,2176]{0,1:T(8,128)(2,1)S(1)}, bf16[128,2176]{0,1:T(8,128)(2,1)S(1)}, u32[]{:S(2)}, u32[]{:S(2)}) collective-permute-start(bf16[128,2176]{0,1:T(8,128)(2,1)S(1)} %pad_maximum_fusion.1), channel_id=1, source_target_pairs={{0,1},{1,2},{2,3},{3,4},{4,5},{5,6},{6,7},{7,8},{8,9},{9,10},{10,1... | collective-permute-start | bytes 1671176 | tf_op jit(solution)/shard_map/ppermute | solution.py:32
  10.9 29.1 %collective-permute-start = (bf16[128,2176]{0,1:T(8,128)(2,1)S(1)}, bf16[128,2176]{0,1:T(8,128)(2,1)S(1)}, u32[]{:S(2)}, u32[]{:S(2)}) collective-permute-start(bf16[128,2176]{0,1:T(8,128)(2,1)S(1)} %pad_maximum_fusion.1), channel_id=1, source_target_pairs={{0,31},{1,0},{2,1},{3,2},{4,3},{5,4},{6,5},{7,6},{8,7},{9,8},{10,9... | collective-permute-start | bytes 1671176 | tf_op jit(solution)/shard_map/ppermute | solution.py:32
  38.1 75.4 %copy-start.21 = (bf16[128,2176]{0,1:T(8,128)(2,1)}, bf16[128,2176]{0,1:T(8,128)(2,1)S(1)}, u32[]{:S(2)}) copy-start(bf16[128,2176]{0,1:T(8,128)(2,1)S(1)} %collective-permute-done.9) | copy-start | bytes 1671172
  38.1 16.0 %collective-permute-start.10 = (bf16[128,2176]{0,1:T(8,128)(2,1)S(1)}, bf16[128,2176]{0,1:T(8,128)(2,1)S(1)}, u32[]{:S(2)}, u32[]{:S(2)}) collective-permute-start(bf16[128,2176]{0,1:T(8,128)(2,1)S(1)} %collective-permute-done.9), channel_id=1, source_target_pairs={{0,1},{1,2},{2,3},{3,4},{4,5},{5,6},{6,7},{7,8},{8,9},{9,10},{10,1... | collective-permute-start | bytes 1671176 | tf_op jit(solution)/shard_map/ppermute | solution.py:32
  40.8 15.2 %collective-permute-start.1 = (bf16[128,2176]{0,1:T(8,128)(2,1)S(1)}, bf16[128,2176]{0,1:T(8,128)(2,1)S(1)}, u32[]{:S(2)}, u32[]{:S(2)}) collective-permute-start(bf16[128,2176]{0,1:T(8,128)(2,1)S(1)} %collective-permute-done), channel_id=1, source_target_pairs={{0,31},{1,0},{2,1},{3,2},{4,3},{5,4},{6,5},{7,6},{8,7},{9,8},{10,9... | collective-permute-start | bytes 1671176 | tf_op jit(solution)/shard_map/ppermute | solution.py:32
  54.1 71.2 %copy-start.25 = (bf16[128,2176]{0,1:T(8,128)(2,1)}, bf16[128,2176]{0,1:T(8,128)(2,1)S(1)}, u32[]{:S(2)}) copy-start(bf16[128,2176]{0,1:T(8,128)(2,1)S(1)} %collective-permute-done.10) | copy-start | bytes 1671172
  54.1 15.2 %collective-permute-start.11 = (bf16[128,2176]{0,1:T(8,128)(2,1)S(1)}, bf16[128,2176]{0,1:T(8,128)(2,1)S(1)}, u32[]{:S(2)}, u32[]{:S(2)}) collective-permute-start(bf16[128,2176]{0,1:T(8,128)(2,1)S(1)} %collective-permute-done.10), channel_id=1, source_target_pairs={{0,1},{1,2},{2,3},{3,4},{4,5},{5,6},{6,7},{7,8},{8,9},{9,10},{10,1... | collective-permute-start | bytes 1671176 | tf_op jit(solution)/shard_map/ppermute | solution.py:32
  56.9 14.7 %collective-permute-start.2 = (bf16[128,2176]{0,1:T(8,128)(2,1)S(1)}, bf16[128,2176]{0,1:T(8,128)(2,1)S(1)}, u32[]{:S(2)}, u32[]{:S(2)}) collective-permute-start(bf16[128,2176]{0,1:T(8,128)(2,1)S(1)} %collective-permute-done.1), channel_id=1, source_target_pairs={{0,31},{1,0},{2,1},{3,2},{4,3},{5,4},{6,5},{7,6},{8,7},{9,8},{10,9... | collective-permute-start | bytes 1671176 | tf_op jit(solution)/shard_map/ppermute | solution.py:32
  69.3 56.0 %copy-start.27 = (bf16[128,2176]{0,1:T(8,128)(2,1)}, bf16[128,2176]{0,1:T(8,128)(2,1)S(1)}, u32[]{:S(2)}) copy-start(bf16[128,2176]{0,1:T(8,128)(2,1)S(1)} %collective-permute-done.11) | copy-start | bytes 1671172
  69.3 14.3 %collective-permute-start.12 = (bf16[128,2176]{0,1:T(8,128)(2,1)S(1)}, bf16[128,2176]{0,1:T(8,128)(2,1)S(1)}, u32[]{:S(2)}, u32[]{:S(2)}) collective-permute-start(bf16[128,2176]{0,1:T(8,128)(2,1)S(1)} %collective-permute-done.11), channel_id=1, source_target_pairs={{0,1},{1,2},{2,3},{3,4},{4,5},{5,6},{6,7},{7,8},{8,9},{9,10},{10,1... | collective-permute-start | bytes 1671176 | tf_op jit(solution)/shard_map/ppermute | solution.py:32
  72.4 14.0 %collective-permute-start.3 = (bf16[128,2176]{0,1:T(8,128)(2,1)S(1)}, bf16[128,2176]{0,1:T(8,128)(2,1)S(1)}, u32[]{:S(2)}, u32[]{:S(2)}) collective-permute-start(bf16[128,2176]{0,1:T(8,128)(2,1)S(1)} %collective-permute-done.2), channel_id=1, source_target_pairs={{0,31},{1,0},{2,1},{3,2},{4,3},{5,4},{6,5},{7,6},{8,7},{9,8},{10,9... | collective-permute-start | bytes 1671176 | tf_op jit(solution)/shard_map/ppermute | solution.py:32
  83.6 41.7 %copy-start.29 = (bf16[128,2176]{0,1:T(8,128)(2,1)}, bf16[128,2176]{0,1:T(8,128)(2,1)S(1)}, u32[]{:S(2)}) copy-start(bf16[128,2176]{0,1:T(8,128)(2,1)S(1)} %collective-permute-done.12) | copy-start | bytes 1671172
  83.6 13.5 %collective-permute-start.13 = (bf16[128,2176]{0,1:T(8,128)(2,1)S(1)}, bf16[128,2176]{0,1:T(8,128)(2,1)S(1)}, u32[]{:S(2)}, u32[]{:S(2)}) collective-permute-start(bf16[128,2176]{0,1:T(8,128)(2,1)S(1)} %collective-permute-done.12), channel_id=1, source_target_pairs={{0,1},{1,2},{2,3},{3,4},{4,5},{5,6},{6,7},{7,8},{8,9},{9,10},{10,1... | collective-permute-start | bytes 1671176 | tf_op jit(solution)/shard_map/ppermute | solution.py:32
  87.2 13.2 %collective-permute-start.4 = (bf16[128,2176]{0,1:T(8,128)(2,1)S(1)}, bf16[128,2176]{0,1:T(8,128)(2,1)S(1)}, u32[]{:S(2)}, u32[]{:S(2)}) collective-permute-start(bf16[128,2176]{0,1:T(8,128)(2,1)S(1)} %collective-permute-done.3), channel_id=1, source_target_pairs={{0,31},{1,0},{2,1},{3,2},{4,3},{5,4},{6,5},{7,6},{8,7},{9,8},{10,9... | collective-permute-start | bytes 1671176 | tf_op jit(solution)/shard_map/ppermute | solution.py:32
  97.1 28.2 %copy-start.31 = (bf16[128,2176]{0,1:T(8,128)(2,1)}, bf16[128,2176]{0,1:T(8,128)(2,1)S(1)}, u32[]{:S(2)}) copy-start(bf16[128,2176]{0,1:T(8,128)(2,1)S(1)} %collective-permute-done.13) | copy-start | bytes 1671172
  97.1 12.6 %collective-permute-start.14 = (bf16[128,2176]{0,1:T(8,128)(2,1)S(1)}, bf16[128,2176]{0,1:T(8,128)(2,1)S(1)}, u32[]{:S(2)}, u32[]{:S(2)}) collective-permute-start(bf16[128,2176]{0,1:T(8,128)(2,1)S(1)} %collective-permute-done.13), channel_id=1, source_target_pairs={{0,1},{1,2},{2,3},{3,4},{4,5},{5,6},{6,7},{7,8},{8,9},{9,10},{10,1... | collective-permute-start | bytes 1671176 | tf_op jit(solution)/shard_map/ppermute | solution.py:32
  101.2 12.3 %collective-permute-start.5 = (bf16[128,2176]{0,1:T(8,128)(2,1)S(1)}, bf16[128,2176]{0,1:T(8,128)(2,1)S(1)}, u32[]{:S(2)}, u32[]{:S(2)}) collective-permute-start(bf16[128,2176]{0,1:T(8,128)(2,1)S(1)} %collective-permute-done.4), channel_id=1, source_target_pairs={{0,31},{1,0},{2,1},{3,2},{4,3},{5,4},{6,5},{7,6},{8,7},{9,8},{10,9... | collective-permute-start | bytes 1671176 | tf_op jit(solution)/shard_map/ppermute | solution.py:32
  109.7 15.6 %copy-start.33 = (bf16[128,2176]{0,1:T(8,128)(2,1)}, bf16[128,2176]{0,1:T(8,128)(2,1)S(1)}, u32[]{:S(2)}) copy-start(bf16[128,2176]{0,1:T(8,128)(2,1)S(1)} %collective-permute-done.14) | copy-start | bytes 1671172
  109.7 11.6 %collective-permute-start.15 = (bf16[128,2176]{0,1:T(8,128)(2,1)S(1)}, bf16[128,2176]{0,1:T(8,128)(2,1)}, u32[]{:S(2)}, u32[]{:S(2)}) collective-permute-start(bf16[128,2176]{0,1:T(8,128)(2,1)S(1)} %collective-permute-done.14), channel_id=1, source_target_pairs={{0,1},{1,2},{2,3},{3,4},{4,5},{5,6},{6,7},{7,8},{8,9},{9,10},{10,1... | collective-permute-start | bytes 1671176 | tf_op jit(solution)/shard_map/ppermute | solution.py:32
  113.5 5.3 %copy-start.23 = (bf16[128,2176]{0,1:T(8,128)(2,1)}, bf16[128,2176]{0,1:T(8,128)(2,1)S(1)}, u32[]{:S(2)}) copy-start(bf16[128,2176]{0,1:T(8,128)(2,1)S(1)} %collective-permute-done.5) | copy-start | bytes 1671172
  113.5 11.8 %collective-permute-start.6 = (bf16[128,2176]{0,1:T(8,128)(2,1)S(1)}, bf16[128,2176]{0,1:T(8,128)(2,1)}, u32[]{:S(2)}, u32[]{:S(2)}) collective-permute-start(bf16[128,2176]{0,1:T(8,128)(2,1)S(1)} %collective-permute-done.5), channel_id=1, source_target_pairs={{0,31},{1,0},{2,1},{3,2},{4,3},{5,4},{6,5},{7,6},{8,7},{9,8},{10,9... | collective-permute-start | bytes 1671176 | tf_op jit(solution)/shard_map/ppermute | solution.py:32
  121.3 12.1 %collective-permute-start.16 = (bf16[128,2176]{0,1:T(8,128)(2,1)}, bf16[128,2176]{0,1:T(8,128)(2,1)}, u32[]{:S(2)}, u32[]{:S(2)}) collective-permute-start(bf16[128,2176]{0,1:T(8,128)(2,1)} %collective-permute-done.15), channel_id=1, source_target_pairs={{0,1},{1,2},{2,3},{3,4},{4,5},{5,6},{6,7},{7,8},{8,9},{9,10},{10,1... | collective-permute-start | bytes 1671176 | tf_op jit(solution)/shard_map/ppermute | solution.py:32
  125.3 12.3 %collective-permute-start.7 = (bf16[128,2176]{0,1:T(8,128)(2,1)}, bf16[128,2176]{0,1:T(8,128)(2,1)}, u32[]{:S(2)}, u32[]{:S(2)}) collective-permute-start(bf16[128,2176]{0,1:T(8,128)(2,1)} %collective-permute-done.6), channel_id=1, source_target_pairs={{0,31},{1,0},{2,1},{3,2},{4,3},{5,4},{6,5},{7,6},{8,7},{9,8},{10,9... | collective-permute-start | bytes 1671176 | tf_op jit(solution)/shard_map/ppermute | solution.py:32
  133.4 12.8 %collective-permute-start.17 = (bf16[128,2176]{0,1:T(8,128)(2,1)}, bf16[128,2176]{0,1:T(8,128)(2,1)S(1)}, u32[]{:S(2)}, u32[]{:S(2)}) collective-permute-start(bf16[128,2176]{0,1:T(8,128)(2,1)} %collective-permute-done.16), channel_id=1, source_target_pairs={{0,1},{1,2},{2,3},{3,4},{4,5},{5,6},{6,7},{7,8},{8,9},{9,10},{10,1... | collective-permute-start | bytes 1671176 | tf_op jit(solution)/shard_map/ppermute | solution.py:32
  137.6 13.4 %collective-permute-start.8 = (bf16[128,2176]{0,1:T(8,128)(2,1)}, bf16[128,2176]{0,1:T(8,128)(2,1)S(1)}, u32[]{:S(2)}, u32[]{:S(2)}) collective-permute-start(bf16[128,2176]{0,1:T(8,128)(2,1)} %collective-permute-done.7), channel_id=1, source_target_pairs={{0,31},{1,0},{2,1},{3,2},{4,3},{5,4},{6,5},{7,6},{8,7},{9,8},{10,9... | collective-permute-start | bytes 1671176 | tf_op jit(solution)/shard_map/ppermute | solution.py:32
  146.2 13.9 %copy-start.5 = (bf16[128,2176]{0,1:T(8,128)(2,1)}, bf16[128,2176]{0,1:T(8,128)(2,1)S(1)}, u32[]{:S(2)}) copy-start(bf16[128,2176]{0,1:T(8,128)(2,1)S(1)} %collective-permute-done.17) | copy-start | bytes 1671172
  153.1 5.2 %copy-start.34 = (bf16[128,2176]{0,1:T(8,128)(2,1)S(1)}, bf16[128,2176]{0,1:T(8,128)(2,1)}, u32[]{:S(2)}) copy-start(bf16[128,2176]{0,1:T(8,128)(2,1)} %copy-done.33) | copy-start | bytes 1671172
  155.3 4.6 %copy-start.42 = (bf16[304,128]{1,0:T(8,128)(2,1)}, bf16[304,128]{1,0:T(8,128)(2,1)S(1)}, u32[]{:S(2)}) copy-start(bf16[304,128]{1,0:T(8,128)(2,1)S(1)} %fusion.26) | copy-start | bytes 233476
  163.4 7.5 %copy-start.48 = (pred[48]{0:T(512)(128)(4,1)S(1)}, pred[48]{0:T(512)(128)(4,1)}, u32[]{:S(2)}) copy-start(pred[48]{0:T(512)(128)(4,1)} %compare_and_fusion.1) | copy-start | bytes 148
  163.4 7.5 %copy-start.49 = (s32[48]{0:T(128)S(1)}, s32[48]{0:T(128)}, u32[]{:S(2)}) copy-start(s32[48]{0:T(128)} %get-tuple-element.37) | copy-start | bytes 580
  168.1 36.3 %collective-permute-start.21 = (bf16[64,2048]{1,0:T(8,128)(2,1)}, bf16[64,2048]{1,0:T(8,128)(2,1)}, u32[]{:S(2)}, u32[]{:S(2)}) collective-permute-start(bf16[64,2048]{1,0:T(8,128)(2,1)} %convolution_convert_fusion.2), channel_id=1, source_target_pairs={{0,4},{1,5},{2,6},{3,7},{4,8},{5,9},{6,10},{7,11},{8,12},{9,13},{1... | collective-permute-start | bytes 786440 | tf_op jit(solution)/shard_map/ppermute | solution.py:32
  173.0 27.0 %collective-permute-start.18 = (bf16[48,2048]{1,0:T(8,128)(2,1)}, bf16[48,2048]{1,0:T(8,128)(2,1)}, u32[]{:S(2)}, u32[]{:S(2)}) collective-permute-start(bf16[48,2048]{1,0:T(8,128)(2,1)} %convolution_convert_fusion.4), channel_id=1, source_target_pairs={{0,28},{1,29},{2,30},{3,31},{4,0},{5,1},{6,2},{7,3},{8,4},{9,5},{1... | collective-permute-start | bytes 589832 | tf_op jit(solution)/shard_map/ppermute | solution.py:32
  183.4 5.0 %copy-start.16 = (bf16[128,2176]{0,1:T(8,128)(2,1)S(1)}, bf16[128,2176]{0,1:T(8,128)(2,1)}, u32[]{:S(2)}) copy-start(bf16[128,2176]{0,1:T(8,128)(2,1)} %copy-done.15) | copy-start | bytes 1671172
  183.4 6.5 %copy-start.18 = (bf16[128,2176]{0,1:T(8,128)(2,1)S(1)}, bf16[128,2176]{0,1:T(8,128)(2,1)}, u32[]{:S(2)}) copy-start(bf16[128,2176]{0,1:T(8,128)(2,1)} %copy-done.17) | copy-start | bytes 1671172
  184.4 7.1 %copy-start.20 = (bf16[128,2176]{0,1:T(8,128)(2,1)S(1)}, bf16[128,2176]{0,1:T(8,128)(2,1)}, u32[]{:S(2)}) copy-start(bf16[128,2176]{0,1:T(8,128)(2,1)} %copy-done.19) | copy-start | bytes 1671172
  186.4 6.7 %copy-start.24 = (bf16[128,2176]{0,1:T(8,128)(2,1)S(1)}, bf16[128,2176]{0,1:T(8,128)(2,1)}, u32[]{:S(2)}) copy-start(bf16[128,2176]{0,1:T(8,128)(2,1)} %copy-done.23) | copy-start | bytes 1671172
  191.4 7.1 %copy-start.4 = (bf16[128,2176]{0,1:T(8,128)(2,1)S(1)}, bf16[128,2176]{0,1:T(8,128)(2,1)}, u32[]{:S(2)}) copy-start(bf16[128,2176]{0,1:T(8,128)(2,1)} %copy-done.3) | copy-start | bytes 1671172
  196.5 8.7 %copy-start.39 = (bf16[16,2048]{1,0:T(8,128)(2,1)S(1)}, bf16[16,2048]{1,0:T(8,128)(2,1)}, u32[]{:S(2)}) copy-start(bf16[16,2048]{1,0:T(8,128)(2,1)} %get-tuple-element.26) | copy-start | bytes 196612
  196.5 8.8 %copy-start.40 = (bf16[16,2048]{1,0:T(8,128)(2,1)S(1)}, bf16[16,2048]{1,0:T(8,128)(2,1)}, u32[]{:S(2)}) copy-start(bf16[16,2048]{1,0:T(8,128)(2,1)} %get-tuple-element.27) | copy-start | bytes 196612
  196.5 11.7 %copy-start.7 = (bf16[19,16,768]{2,1,0:T(8,128)(2,1)S(1)}, bf16[19,16,768]{2,1,0:T(8,128)(2,1)}, u32[]{:S(2)}) copy-start(bf16[19,16,768]{2,1,0:T(8,128)(2,1)} %slice.329) | copy-start | bytes 1400836
  200.1 8.2 %copy-start.10 = (bf16[304,2048]{1,0:T(8,128)(2,1)S(1)}, bf16[304,2048]{1,0:T(8,128)(2,1)}, u32[]{:S(2)}) copy-start(bf16[304,2048]{1,0:T(8,128)(2,1)} %fusion.6) | copy-start | bytes 3735556
  201.1 9.2 %collective-permute-start.19 = (bf16[48,2048]{1,0:T(8,128)(2,1)S(1)}, bf16[48,2048]{1,0:T(8,128)(2,1)S(1)}, u32[]{:S(2)}, u32[]{:S(2)}) collective-permute-start(bf16[48,2048]{1,0:T(8,128)(2,1)S(1)} %pad_maximum_fusion.4), channel_id=1, source_target_pairs={{0,30},{1,31},{2,0},{3,1},{4,2},{5,3},{6,4},{7,5},{8,6},{9,7},{10,... | collective-permute-start | bytes 589832 | tf_op jit(solution)/shard_map/ppermute | solution.py:32
  205.3 11.1 %collective-permute-start.22 = (bf16[64,2048]{1,0:T(8,128)(2,1)S(1)}, bf16[64,2048]{1,0:T(8,128)(2,1)S(1)}, u32[]{:S(2)}, u32[]{:S(2)}) collective-permute-start(bf16[64,2048]{1,0:T(8,128)(2,1)S(1)} %pad_maximum_fusion.2), channel_id=1, source_target_pairs={{0,2},{1,3},{2,4},{3,5},{4,6},{5,7},{6,8},{7,9},{8,10},{9,11},{10,... | collective-permute-start | bytes 786440 | tf_op jit(solution)/shard_map/ppermute | solution.py:32
  208.3 8.2 %copy-start.38 = (bf16[16,2048]{1,0:T(8,128)(2,1)S(1)}, bf16[16,2048]{1,0:T(8,128)(2,1)}, u32[]{:S(2)}) copy-start(bf16[16,2048]{1,0:T(8,128)(2,1)} %get-tuple-element.25) | copy-start | bytes 196612
  210.3 11.1 %collective-permute-start.20 = (bf16[48,2048]{1,0:T(8,128)(2,1)S(1)}, bf16[48,2048]{1,0:T(8,128)(2,1)S(1)}, u32[]{:S(2)}, u32[]{:S(2)}) collective-permute-start(bf16[48,2048]{1,0:T(8,128)(2,1)S(1)} %pad_maximum_fusion.5), channel_id=1, source_target_pairs={{0,31},{1,0},{2,1},{3,2},{4,3},{5,4},{6,5},{7,6},{8,7},{9,8},{10,9... | collective-permute-start | bytes 589832 | tf_op jit(solution)/shard_map/ppermute | solution.py:32
  216.5 12.9 %collective-permute-start.23 = (bf16[64,2048]{1,0:T(8,128)(2,1)S(1)}, bf16[64,2048]{1,0:T(8,128)(2,1)S(1)}, u32[]{:S(2)}, u32[]{:S(2)}) collective-permute-start(bf16[64,2048]{1,0:T(8,128)(2,1)S(1)} %pad_maximum_fusion.3), channel_id=1, source_target_pairs={{0,1},{1,2},{2,3},{3,4},{4,5},{5,6},{6,7},{7,8},{8,9},{9,10},{10,1... | collective-permute-start | bytes 786440 | tf_op jit(solution)/shard_map/ppermute | solution.py:32
  237.2 14.8 %copy-start.45 = (s32[128,8]{0,1:T(8,128)S(1)}, s32[128,8]{0,1:T(8,128)}, u32[]{:S(2)}) copy-start(s32[128,8]{0,1:T(8,128)} %param.19) | copy-start | bytes 12292
  237.2 14.8 %copy-start.50 = (f32[128,8]{0,1:T(8,128)S(1)}, f32[128,8]{0,1:T(8,128)}, u32[]{:S(2)}) copy-start(f32[128,8]{0,1:T(8,128)} %param.20) | copy-start | bytes 12292
  237.2 49.6 %copy-start.44 = (f32[32,128]{1,0:T(8,128)S(1)}, f32[32,128]{1,0:T(8,128)}, u32[]{:S(2)}) copy-start(f32[32,128]{1,0:T(8,128)} %copy-done.43) | copy-start | bytes 49156
  239.3 61.2 %collective-permute-start.24 = (bf16[16,24,2048]{2,1,0:T(8,128)(2,1)}, bf16[16,24,2048]{2,1,0:T(8,128)(2,1)}, u32[]{:S(2)}, u32[]{:S(2)}) collective-permute-start(bf16[16,24,2048]{2,1,0:T(8,128)(2,1)} %dynamic-slice_bitcast_fusion), channel_id=1, source_target_pairs={{0,32},{32,0},{64,96},{96,64},{128,160},{160,128},{192,224},{224,1... | collective-permute-start | bytes 4718600 | tf_op jit(solution)/shard_map/ppermute | solution.py:89
  252.0 34.8 %all-to-all-start = ((f32[32,1,16]{2,1,0:T(1,128)}), f32[32,1,16]{2,1,0:T(1,128)S(1)}, u32[]{:S(2)}, u32[]{:S(2)}) async-start(f32[32,1,16]{2,1,0:T(1,128)} %bitcast.6), calls=%async_computation | async-start | bytes 32768 | tf_op jit(solution)/shard_map/all_to_all | solution.py:188
  291.8 24.1 %all-to-all-start.1 = ((bf16[32,64,128]{2,1,0:T(8,128)(2,1)}), bf16[32,64,128]{2,1,0:T(8,128)(2,1)}, u32[]{:S(2)}, u32[]{:S(2)}) async-start(bf16[32,64,128]{2,1,0:T(8,128)(2,1)} %bitcast.89), calls=%async_computation.1 | async-start | bytes 1048576 | tf_op jit(solution)/shard_map/all_to_all | solution.py:21
  303.0 11.7 %copy-start.2 = (bf16[16,24,2048]{2,1,0:T(8,128)(2,1)}, bf16[16,24,2048]{2,1,0:T(8,128)(2,1)S(1)}, u32[]{:S(2)}) copy-start(bf16[16,24,2048]{2,1,0:T(8,128)(2,1)S(1)} %fusion) | copy-start | bytes 4718596
  303.0 11.7 %copy-start.35 = (bf16[304,768]{1,0:T(8,128)(2,1)S(1)}, bf16[304,768]{1,0:T(8,128)(2,1)}, u32[]{:S(2)}) copy-start(bf16[304,768]{1,0:T(8,128)(2,1)} %get-tuple-element.15) | copy-start | bytes 1400836
  303.0 11.7 %copy-start.36 = (bf16[208,768]{1,0:T(8,128)(2,1)S(1)}, bf16[208,768]{1,0:T(8,128)(2,1)}, u32[]{:S(2)}) copy-start(bf16[208,768]{1,0:T(8,128)(2,1)} %get-tuple-element.17) | copy-start | bytes 958468
  304.0 40.5 %collective-permute-start.25 = (bf16[4,24,2048]{2,1,0:T(8,128)(2,1)}, bf16[4,24,2048]{2,1,0:T(8,128)(2,1)}, u32[]{:S(2)}, u32[]{:S(2)}) collective-permute-start(bf16[4,24,2048]{2,1,0:T(8,128)(2,1)} %get-tuple-element.12), channel_id=1, source_target_pairs={{0,64},{32,96},{64,128},{96,160},{128,192},{160,224},{192,0},{224,... | collective-permute-start | bytes 1179656 | tf_op jit(solution)/shard_map/ppermute | solution.py:89
  307.3 37.2 %collective-permute-start.26 = (bf16[4,24,2048]{2,1,0:T(8,128)(2,1)}, bf16[4,24,2048]{2,1,0:T(8,128)(2,1)}, u32[]{:S(2)}, u32[]{:S(2)}) collective-permute-start(bf16[4,24,2048]{2,1,0:T(8,128)(2,1)} %get-tuple-element.14), channel_id=1, source_target_pairs={{0,128},{32,160},{64,192},{96,224},{128,0},{160,32},{192,64},{224,... | collective-permute-start | bytes 1179656 | tf_op jit(solution)/shard_map/ppermute | solution.py:89
  311.6 32.9 %collective-permute-start.27 = (bf16[4,24,2048]{2,1,0:T(8,128)(2,1)S(1)}, bf16[4,24,2048]{2,1,0:T(8,128)(2,1)}, u32[]{:S(2)}, u32[]{:S(2)}) collective-permute-start(bf16[4,24,2048]{2,1,0:T(8,128)(2,1)S(1)} %get-tuple-element.13), channel_id=1, source_target_pairs={{0,192},{32,224},{64,0},{96,32},{128,64},{160,96},{192,128},{224,1... | collective-permute-start | bytes 1179656 | tf_op jit(solution)/shard_map/ppermute | solution.py:89
  319.3 24.5 %all-to-all-start.2 = ((bf16[32,2,128]{2,1,0:T(2,128)(2,1)}), bf16[32,2,128]{2,1,0:T(2,128)(2,1)S(1)}, u32[]{:S(2)}, u32[]{:S(2)}) async-start(bf16[32,2,128]{2,1,0:T(2,128)(2,1)} %reshape.67), calls=%async_computation.2 | async-start | bytes 32768 | tf_op jit(solution)/shard_map/all_to_all | solution.py:21
  344.5 12.2 %copy-start.41 = (bf16[32,4,64]{2,1,0:T(4,128)(2,1)S(1)}, bf16[32,4,64]{2,1,0:T(4,128)(2,1)}, u32[]{:S(2)}) copy-start(bf16[32,4,64]{2,1,0:T(4,128)(2,1)} %reshape.68) | copy-start | bytes 49156
  346.2 11.2 %collective-permute-start.28 = (bf16[24,2048]{1,0:T(8,128)(2,1)S(1)}, bf16[24,2048]{1,0:T(8,128)(2,1)S(1)}, u32[]{:S(2)}, u32[]{:S(2)}) collective-permute-start(bf16[24,2048]{1,0:T(8,128)(2,1)S(1)} %get-tuple-element.19), channel_id=1, source_target_pairs={{0,256},{32,288},{64,320},{96,352},{128,384},{160,416},{192,448},{... | collective-permute-start | bytes 294920 | tf_op jit(solution)/shard_map/ppermute | solution.py:89
  349.3 8.1 %collective-permute-start.29 = (bf16[24,2048]{1,0:T(8,128)(2,1)S(1)}, bf16[24,2048]{1,0:T(8,128)(2,1)S(1)}, u32[]{:S(2)}, u32[]{:S(2)}) collective-permute-start(bf16[24,2048]{1,0:T(8,128)(2,1)S(1)} %get-tuple-element.21), channel_id=1, source_target_pairs={{0,512},{32,544},{64,576},{96,608},{128,640},{160,672},{192,704},{... | collective-permute-start | bytes 294920 | tf_op jit(solution)/shard_map/ppermute | solution.py:89
  353.6 6.3 %collective-permute-start.30 = (bf16[24,2048]{1,0:T(8,128)(2,1)S(1)}, bf16[24,2048]{1,0:T(8,128)(2,1)S(1)}, u32[]{:S(2)}, u32[]{:S(2)}) collective-permute-start(bf16[24,2048]{1,0:T(8,128)(2,1)S(1)} %get-tuple-element.20), channel_id=1, source_target_pairs={{0,768},{32,800},{64,832},{96,864},{128,896},{160,928},{192,960},{... | collective-permute-start | bytes 294920 | tf_op jit(solution)/shard_map/ppermute | solution.py:89
  (21 other events, 34.1 us)
